TPU v7x, 128 devices: a whole 4x4x4 slice. The times are simulated.
128 devices in a mesh: seq: 8 (over z_hi, x), exp: 16 (over z_lo, y, core).
Axes of the slice: x: 4, y: 4, z: 4 (z_hi: 2, z_lo: 2; z = z_hi * 2 + z_lo), core: 2. Of those that a mesh axis runs over, the one named last changes fastest.
Arguments:
- queries: bfloat16 [16384, 3072], P(('seq', 'exp')), may hold values from -123 to 123
- keys: bfloat16 [16384, 512], P(('seq', 'exp')), may hold values from -6 to 6
- values: bfloat16 [16384, 512], P(('seq', 'exp')), may hold values from -9 to 9
- residual: bfloat16 [16384, 6144], P(('seq', 'exp')), may hold values from -51 to 51
- proj_weight: bfloat16 [3072, 6144], P('seq', 'exp'), may hold values from -0.109375 to 0.109375
- norm_gain: bfloat16 [6144], replicated, may hold values from 0.099609375 to 1.8984375
- router: bfloat16 [6144, 8], replicated, may hold values from -0.078125 to 0.078125
- expert_ids: int32 [16384, 2], P(('seq', 'exp')), may hold values from 0 to 7, all different within a row; in each aligned block of 128 rows (0 to 127, 128 to 255, ...) at most 33 rows name the same one
- u_gate_up: bfloat16 [16, 3072, 1024], P('exp'), may hold values from -0.078125 to 0.078125
- v_gate_up: bfloat16 [16, 2, 512, 4096], P('exp'), may hold values from -0.25 to 0.25
- u_down: bfloat16 [16, 4096, 512], P('exp'), may hold values from -0.0625 to 0.0625
- v_down: bfloat16 [16, 512, 3072], P('exp'), may hold values from -0.25 to 0.25
Outputs:
- layer_out: bfloat16 [16384, 6144], P(('seq', 'exp'))
Inputs may be any that keep to these rules, and one draw needn't show every extreme that they name: `expert_ids`: the two experts of a token differ. Among the tokens of one device no expert is named more than 33 times, and in some devices' tokens some expert is named exactly 33 times.
All inputs are finite; a program needn't handle non-finite values.
Results may differ from a plain program's by a relative error of at most 0.02.
Values may be sent and summed in bfloat16 or wider, within the bound.
A program may use at most 192 MiB of HBM per device.

v0:
```python
import jax
import jax.numpy as jnp
from jax import lax
from jax.sharding import PartitionSpec as P

D = 6144
HEADS = 24
KV_HEADS = 4
HEAD_DIM = 128
GROUP_HEADS = 3
EXPERTS = 8
RANK = 512
TOK_DEV = 128
CAP = 33
EPS = 1e-05


def in_one_piece(arrays, axis, split_dim, concat_dim, along):
    both = jnp.concatenate(arrays, axis=along)
    out, at, finished = (
        lax.all_to_all(both, axis, split_axis=split_dim, concat_axis=concat_dim, tiled=True),
        0,
        [],
    )
    for a in arrays:
        finished.append(lax.slice_in_dim(out, at, at + a.shape[along], axis=along))
        at += a.shape[along]
    return tuple(finished)


def swapped(x, axis, distance):
    return lax.ppermute(x, axis, [(i, i ^ 1 << distance) for i in range(lax.axis_size(axis))])


def passed_along(value, axis, steps):
    count = lax.axis_size(axis)
    pairs = [(source, (source + steps) % count) for source in range(count)]
    return lax.ppermute(value, axis, pairs)


def attend(current, query_rows, key_rows, value_rows, allowed):
    row_max, row_sum, weighted = current
    scores = jnp.einsum("qhd,kd->qhk", query_rows, key_rows, preferred_element_type=jnp.float32)
    scores = scores * HEAD_DIM ** (-0.5)
    if allowed is not None:
        scores = jnp.where(allowed[:, None, :], scores, -jnp.inf)
    new_max = jnp.maximum(row_max, jnp.max(scores, axis=-1))
    fading = jnp.exp(row_max - new_max)
    exp_terms = jnp.exp(scores - new_max[..., None])
    row_sum = row_sum * fading + jnp.sum(exp_terms, axis=-1)
    update = jnp.einsum(
        "qhk,kd->qhd",
        exp_terms.astype(jnp.bfloat16),
        value_rows,
        preferred_element_type=jnp.float32,
    )
    weighted = weighted * fading[..., None] + update
    return (new_max, row_sum, weighted)


def fresh_states(count_rows):
    query_step = min(512, count_rows)
    states = [
        (
            jnp.full((query_step, GROUP_HEADS), -1e30, jnp.float32),
            jnp.zeros((query_step, GROUP_HEADS), jnp.float32),
            jnp.zeros((query_step, GROUP_HEADS, HEAD_DIM), jnp.float32),
        )
    ]
    return states


def attend_all(states, query_rows, query_pos, key_rows, value_rows, key_pos, mode):
    current = states[0]
    if mode == "open":
        current = attend(current, query_rows, key_rows, value_rows, None)
    else:
        allowed = key_pos[None, :] <= query_pos[:, None]
        current = attend(current, query_rows, key_rows, value_rows, allowed)
    updated = [current]
    return updated


def pick_states(stacked, which):
    return [
        tuple((lax.dynamic_index_in_dim(member, which, 0, keepdims=False) for member in tile))
        for tile in stacked
    ]


def put_states(stacked, which, fresh):
    return [
        tuple(
            (
                lax.dynamic_update_index_in_dim(member, newer, which, 0)
                for member, newer in zip(tile, new_tile)
            )
        )
        for tile, new_tile in zip(stacked, fresh)
    ]


def finish(states):
    results = [weighted / row_sum[..., None] for row_max, row_sum, weighted in states]
    joined = results[0].astype(jnp.bfloat16)
    return joined.reshape(joined.shape[0], GROUP_HEADS * HEAD_DIM)


def per_device(
    queries,
    keys,
    values,
    residual,
    proj_weight,
    norm_gain,
    router,
    expert_ids,
    u_gate_up,
    v_gate_up,
    u_down,
    v_down,
):
    seq_count = lax.axis_size("seq")
    exp_count = lax.axis_size("exp")
    seq_index = lax.axis_index("seq")
    exp_index = lax.axis_index("exp")
    group_count = HEADS // GROUP_HEADS
    split_count = exp_count // group_count
    group_width = GROUP_HEADS * HEAD_DIM
    token_rows = TOK_DEV // split_count
    block_len = TOK_DEV * exp_count
    query_count = exp_count * token_rows
    per_kv = group_count // KV_HEADS
    half_index = exp_index // group_count
    query_send = queries.reshape(token_rows, exp_count, group_width)
    kv_shape = (TOK_DEV, split_count, KV_HEADS, per_kv, HEAD_DIM)
    key_send = jnp.broadcast_to(keys.reshape(TOK_DEV, 1, KV_HEADS, 1, HEAD_DIM), kv_shape).reshape(
        TOK_DEV, exp_count, HEAD_DIM
    )
    value_send = jnp.broadcast_to(
        values.reshape(TOK_DEV, 1, KV_HEADS, 1, HEAD_DIM), kv_shape
    ).reshape(TOK_DEV, exp_count, HEAD_DIM)
    query_got, key_got, value_got = (
        lax.all_to_all(query_send, "exp", split_axis=1, concat_axis=0, tiled=True),
        *in_one_piece((key_send, value_send), "exp", 1, 0, 2),
    )
    query_local = query_got.reshape(query_count, GROUP_HEADS, HEAD_DIM)
    key_local = key_got.reshape(block_len, HEAD_DIM)
    value_local = value_got.reshape(block_len, HEAD_DIM)
    row_ids = jnp.arange(query_count, dtype=jnp.int32)
    in_block = row_ids // token_rows * TOK_DEV + row_ids % token_rows * split_count + half_index
    key_offsets = jnp.arange(block_len, dtype=jnp.int32)
    half_q = query_count // 2
    half_k = block_len // 2
    query_near = query_local[:half_q]
    query_far = query_local[half_q:]
    key_far = key_local[half_k:]
    value_far = value_local[half_k:]
    for bit_index in range(seq_count.bit_length() - 1):
        query_far, key_far, value_far = swapped((query_far, key_far, value_far), "seq", bit_index)
    mirror_index = seq_count - 1 - seq_index
    near_pos = seq_index * block_len + in_block[:half_q]
    far_pos = mirror_index * block_len + in_block[half_q:]
    query_pair = jnp.stack([query_near, query_far])
    pair_states = [
        tuple((jnp.stack([member, member]) for member in tile)) for tile in fresh_states(half_q)
    ]
    held_blocks = (key_local[:half_k], value_local[:half_k], key_far, value_far)
    for step_index in range(seq_count):
        if step_index + 1 < seq_count:
            arrived = passed_along(
                (held_blocks[0], held_blocks[1], held_blocks[2], held_blocks[3]), "seq", 1
            )
        source = (seq_index - step_index) % seq_count
        low_keys, low_values, high_keys, high_values = held_blocks
        if step_index == 0:
            low_pos = source * block_len + key_offsets[:half_k]
            high_pos = (seq_count - 1 - source) * block_len + half_k + key_offsets[:half_k]
            near_now = pick_states(pair_states, 0)
            near_now = attend_all(
                near_now, query_near, near_pos, low_keys, low_values, low_pos, "masked"
            )
            pair_states = put_states(pair_states, 0, near_now)
            far_now = pick_states(pair_states, 1)
            far_now = attend_all(
                far_now, query_far, far_pos, high_keys, high_values, high_pos, "masked"
            )
            pair_states = put_states(pair_states, 1, far_now)
        else:
            first_low = source <= seq_index
            first_slot = jnp.where(first_low, 0, 1).astype(jnp.int32)
            key_pick = jnp.where(first_low, low_keys, high_keys)
            value_pick = jnp.where(first_low, low_values, high_values)
            query_pick = lax.dynamic_index_in_dim(query_pair, first_slot, 0, keepdims=False)
            picked_states = attend_all(
                pick_states(pair_states, first_slot),
                query_pick,
                None,
                key_pick,
                value_pick,
                None,
                "open",
            )
            pair_states = put_states(pair_states, first_slot, picked_states)
        second_high = source >= seq_count - seq_index
        second_slot = jnp.where(second_high, 0, 1).astype(jnp.int32)
        key_pick = jnp.where(second_high, high_keys, low_keys)
        value_pick = jnp.where(second_high, high_values, low_values)
        query_pick = lax.dynamic_index_in_dim(query_pair, second_slot, 0, keepdims=False)
        picked_states = attend_all(
            pick_states(pair_states, second_slot),
            query_pick,
            None,
            key_pick,
            value_pick,
            None,
            "open",
        )
        pair_states = put_states(pair_states, second_slot, picked_states)
        if step_index + 1 < seq_count:
            held_blocks = arrived
    attended_near = finish(pick_states(pair_states, 0))
    attended_far = finish(pick_states(pair_states, 1))
    for bit_index in range(seq_count.bit_length() - 1):
        attended_far = swapped(attended_far, "seq", bit_index)
    attended = jnp.concatenate([attended_near, attended_far], axis=0)
    weight_rows = lax.all_gather(proj_weight, "seq", axis=0, tiled=True)
    column_count = weight_rows.shape[1]
    blank_sum = jnp.zeros((exp_count, token_rows, split_count, column_count), jnp.float32)
    carried = blank_sum
    shard_piece = lax.all_gather(attended, "exp", axis=0, tiled=True)
    start_row = jnp.int32(0)
    shard_total = shard_piece.shape[0] // query_count
    for shard_index in range(shard_total):
        device_id = start_row // query_count + shard_index
        group_id = device_id % group_count
        half_id = device_id // group_count
        weight_slice = lax.dynamic_slice_in_dim(weight_rows, group_id * group_width, group_width, 0)
        rows_now = shard_piece[shard_index * query_count : (shard_index + 1) * query_count]
        product = jnp.dot(rows_now, weight_slice, preferred_element_type=jnp.float32)
        product = product.reshape(exp_count, token_rows, 1, column_count)
        corner = (0, 0, half_id, 0)
        present = lax.dynamic_slice(carried, corner, (exp_count, token_rows, 1, column_count))
        carried = lax.dynamic_update_slice(carried, present + product, corner)
    projected = carried
    projected = projected.reshape(block_len, column_count)
    attn_block = projected.astype(jnp.bfloat16)
    attn_update = lax.all_to_all(attn_block, "exp", split_axis=0, concat_axis=1, tiled=True)
    stream = residual.astype(jnp.float32) + attn_update.astype(jnp.float32)
    mean_sq = jnp.mean(stream * stream, axis=-1, keepdims=True)
    normed = (stream * lax.rsqrt(mean_sq + EPS) * norm_gain.astype(jnp.float32)).astype(
        jnp.bfloat16
    )
    logits = jnp.dot(normed, router, preferred_element_type=jnp.float32)
    expert_range = jnp.arange(EXPERTS, dtype=jnp.int32)
    picked = (expert_ids[:, :, None] == expert_range[None, None, :]).astype(jnp.float32)
    chosen = jnp.sum(picked * logits[:, None, :], axis=-1)
    mix_first = jax.nn.sigmoid(chosen[:, 0] - chosen[:, 1])
    mix_second = jax.nn.sigmoid(chosen[:, 1] - chosen[:, 0])
    piece_count = exp_count // EXPERTS
    piece_width = D // piece_count
    flat_ids = expert_ids.reshape(TOK_DEV * 2)
    member = (flat_ids[:, None] == expert_range[None, :]).astype(jnp.int32)
    slot_of = jnp.sum((jnp.cumsum(member, axis=0) - 1) * member, axis=1)
    token_of = jnp.arange(TOK_DEV * 2, dtype=jnp.int32) // 2
    slot_range = jnp.arange(CAP, dtype=jnp.int32)
    filled = member[:, :, None] * (slot_of[:, None, None] == slot_range[None, None, :]).astype(
        jnp.int32
    )
    source_token = jnp.sum(filled * token_of[:, None, None], axis=0)
    occupied = jnp.sum(filled, axis=0)
    piece_range = jnp.arange(piece_count, dtype=jnp.int32)
    take_index = source_token[:, None, :] * piece_count + piece_range[None, :, None]
    normed_rows = normed.reshape(TOK_DEV * piece_count, piece_width)
    send_rows = jnp.take(normed_rows, take_index, axis=0) * occupied[:, None, :, None].astype(
        jnp.bfloat16
    )
    send_rows = send_rows.reshape(exp_count, CAP, piece_width)
    dispatched = lax.all_to_all(send_rows, "exp", split_axis=0, concat_axis=0, tiled=True)
    expert_rows = dispatched.reshape(exp_count * CAP, piece_width)
    rank_sum = jnp.dot(expert_rows, u_gate_up[0], preferred_element_type=jnp.float32)
    bit_index = 0
    rank_sum = rank_sum + swapped(rank_sum.astype(jnp.bfloat16), "exp", bit_index).astype(
        rank_sum.dtype
    )
    rank_in = rank_sum.astype(jnp.bfloat16)
    gate_part = jnp.dot(rank_in[:, :RANK], v_gate_up[0, 0], preferred_element_type=jnp.float32)
    up_part = jnp.dot(rank_in[:, RANK:], v_gate_up[0, 1], preferred_element_type=jnp.float32)
    hidden = (jax.nn.silu(gate_part) * up_part).astype(jnp.bfloat16)
    down_sum = jnp.dot(hidden, u_down[0], preferred_element_type=jnp.float32)
    bit_index = 0
    down_sum = down_sum + swapped(down_sum.astype(jnp.bfloat16), "exp", bit_index).astype(
        down_sum.dtype
    )
    expert_out = jnp.dot(
        down_sum.astype(jnp.bfloat16), v_down[0], preferred_element_type=jnp.float32
    ).astype(jnp.bfloat16)
    returned = lax.all_to_all(
        expert_out.reshape(exp_count, CAP, piece_width),
        "exp",
        split_axis=0,
        concat_axis=0,
        tiled=True,
    )
    returned_rows = returned.reshape(exp_count * CAP, piece_width)
    slot_pairs = slot_of.reshape(TOK_DEV, 2)
    fetch_index = (
        expert_ids[:, :, None] * piece_count + piece_range[None, None, :]
    ) * CAP + slot_pairs[:, :, None]
    fetched = jnp.take(returned_rows, fetch_index, axis=0).astype(jnp.float32)
    fetched = fetched.reshape(TOK_DEV, 2, D)
    mixture = mix_first[:, None] * fetched[:, 0] + mix_second[:, None] * fetched[:, 1]
    return (stream + mixture).astype(jnp.bfloat16)


def solution(mesh):
    in_specs = (
        P(("seq", "exp"), None),
        P(("seq", "exp"), None),
        P(("seq", "exp"), None),
        P(("seq", "exp"), None),
        P("seq", "exp"),
        P(),
        P(),
        P(("seq", "exp"), None),
        P("exp", None, None),
        P("exp", None, None, None),
        P("exp", None, None),
        P("exp", None, None),
    )
    out_specs = P(("seq", "exp"), None)
    return jax.shard_map(
        per_device, mesh=mesh, in_specs=in_specs, out_specs=out_specs, check_vma=False
    )
```

profile of v0, /device:TPU:8, one launch (start us, length us, event | category | flops | bytes accessed | tf_op | source)
XLA Modules:
  0.0 711.7 jit_solution(16518140641565439048)
XLA Ops:
  11.1 6.3 all-to-all-start.1
  19.6 8.3 %all-to-all-done.1 = bf16[64,16,384]{2,0,1:T(8,128)(2,1)} async-done(((bf16[64,16,384]{2,0,1:T(8,128)(2,1)}), bf16[64,16,384]{2,0,1:T(8,128)(2,1)}, u32[]{:S(2)}, u32[]{:S(2)}) %all-to-all-start.1) | async-done | bytes 786464 | tf_op jit(solution)/shard_map/all_to_all | solution.py:144
  27.9 7.4 %all-to-all-start = ((bf16[128,16,256]{2,0,1:T(8,128)(2,1)}), bf16[128,16,256]{2,0,1:T(8,128)(2,1)}, u32[]{:S(2)}, u32[]{:S(2)}) async-start(bf16[128,16,256]{2,0,1:T(8,128)(2,1)} %pad_maximum_fusion.1), calls=%async_computation | async-start | bytes 2097152 | tf_op jit(solution)/shard_map/all_to_all | solution.py:21
  55.5 2.6 fusion.36
  59.7 3.3 collective-permute-start.4
  63.1 4.8 collective-permute-done
  67.8 3.2 collective-permute-start.1
  71.0 5.0 collective-permute-done.6
  76.0 3.5 collective-permute-start.7
  80.9 6.5 collective-permute-done.11
  89.9 2.6 fusion.258
  92.5 13.6 %collective-permute-done.1 = bf16[1024,128]{1,0:T(8,128)(2,1)S(1)} collective-permute-done((bf16[1024,128]{1,0:T(8,128)(2,1)S(1)}, bf16[1024,128]{1,0:T(8,128)(2,1)S(1)}, u32[]{:S(2)}, u32[]{:S(2)}) %collective-permute-start.1) | collective-permute-done | bytes 262176 | tf_op jit(solution)/shard_map/ppermute | solution.py:32
  106.1 3.6 collective-permute-start.2
  111.6 3.6 collective-permute-start.8
  116.5 4.6 collective-permute-done.15
  122.1 3.8 collective-permute-start.5
  127.3 8.9 %collective-permute-done.2 = bf16[1024,128]{1,0:T(8,128)(2,1)S(1)} collective-permute-done((bf16[1024,128]{1,0:T(8,128)(2,1)S(1)}, bf16[1024,128]{1,0:T(8,128)(2,1)S(1)}, u32[]{:S(2)}, u32[]{:S(2)}) %collective-permute-start.2) | collective-permute-done | bytes 262176 | tf_op jit(solution)/shard_map/ppermute | solution.py:32
  136.2 5.6 collective-permute-done.8
  144.3 24.7 %collective-permute-done.5 = bf16[512,3,128]{2,0,1:T(8,128)(2,1)S(1)} collective-permute-done((bf16[512,3,128]{2,0,1:T(8,128)(2,1)S(1)}, bf16[512,3,128]{2,0,1:T(8,128)(2,1)S(1)}, u32[]{:S(2)}, u32[]{:S(2)}) %collective-permute-start.5) | collective-permute-done | bytes 393248 | tf_op jit(solution)/shard_map/ppermute | solution.py:32
  188.5 7.0 collective-permute-start.27
  195.5 3.7 collective-permute-done.14
  201.7 3.2 collective-permute-done.16
  211.4 4.7 collective-permute-done.27
  217.7 4.0 collective-permute-done.18
  224.1 3.2 collective-permute-done.20
  233.9 4.7 collective-permute-done.31
  240.2 4.0 collective-permute-done.22
  246.6 3.2 collective-permute-done.24
  255.6 11.0 %collective-permute-done.26 = bf16[1024,128]{1,0:T(8,128)(2,1)S(1)} collective-permute-done((bf16[1024,128]{1,0:T(8,128)(2,1)S(1)}, bf16[1024,128]{1,0:T(8,128)(2,1)S(1)}, u32[]{:S(2)}, u32[]{:S(2)}) %collective-permute-start.26) | collective-permute-done | bytes 262176 | tf_op jit(solution)/shard_map/ppermute | solution.py:38
  276.8 10.7 %collective-permute-done.30 = bf16[1024,128]{1,0:T(8,128)(2,1)S(1)} collective-permute-done((bf16[1024,128]{1,0:T(8,128)(2,1)S(1)}, bf16[1024,128]{1,0:T(8,128)(2,1)S(1)}, u32[]{:S(2)}, u32[]{:S(2)}) %collective-permute-start.30) | collective-permute-done | bytes 262176 | tf_op jit(solution)/shard_map/ppermute | solution.py:38
  296.5 10.5 %collective-permute-done.34 = bf16[1024,128]{1,0:T(8,128)(2,1)S(1)} collective-permute-done((bf16[1024,128]{1,0:T(8,128)(2,1)S(1)}, bf16[1024,128]{1,0:T(8,128)(2,1)S(1)}, u32[]{:S(2)}, u32[]{:S(2)}) %collective-permute-start.34) | collective-permute-done | bytes 262176 | tf_op jit(solution)/shard_map/ppermute | solution.py:38
  316.9 10.4 %collective-permute-done.37 = bf16[512,384]{0,1:T(8,128)(2,1)S(1)} collective-permute-done((bf16[512,384]{0,1:T(8,128)(2,1)S(1)}, bf16[512,384]{0,1:T(8,128)(2,1)S(1)}, u32[]{:S(2)}, u32[]{:S(2)}) %collective-permute-start.37) | collective-permute-done | bytes 393248 | tf_op jit(solution)/shard_map/ppermute | solution.py:32
  327.4 9.3 %collective-permute-done.38 = bf16[512,384]{0,1:T(8,128)(2,1)S(1)} collective-permute-done((bf16[512,384]{0,1:T(8,128)(2,1)S(1)}, bf16[512,384]{0,1:T(8,128)(2,1)S(1)}, u32[]{:S(2)}, u32[]{:S(2)}) %collective-permute-start.38) | collective-permute-done | bytes 393248 | tf_op jit(solution)/shard_map/ppermute | solution.py:32
  336.7 9.2 %collective-permute-done.39 = bf16[512,384]{0,1:T(8,128)(2,1)S(1)} collective-permute-done((bf16[512,384]{0,1:T(8,128)(2,1)S(1)}, bf16[512,384]{0,1:T(8,128)(2,1)S(1)}, u32[]{:S(2)}, u32[]{:S(2)}) %collective-permute-start.39) | collective-permute-done | bytes 393248 | tf_op jit(solution)/shard_map/ppermute | solution.py:32
  348.2 66.8 %all-gather.3.cloned.1.call-done = bf16[16384,384]{0,1:T(8,128)(2,1)} async-done(((bf16[1024,384]{0,1:T(8,128)(2,1)}), bf16[16384,384]{0,1:T(8,128)(2,1)}) %all-gather.3.cloned.1.call-update) | async-done | bytes 12582928 | tf_op jit(solution)/shard_map/all_gather | solution.py:231
  435.2 2.6 fusion.119
  443.6 2.6 constant_dynamic-update-slice_fusion.2
  455.2 2.8 fusion.118
  459.7 5.6 all-to-all-start.2
  465.5 2.6 copy.303
  469.9 16.8 %all-to-all-done.2 = bf16[16,128,384]{2,1,0:T(8,128)(2,1)} async-done(((bf16[16,128,384]{2,1,0:T(8,128)(2,1)}), bf16[16,128,384]{2,1,0:T(8,128)(2,1)}, u32[]{:S(2)}, u32[]{:S(2)}) %all-to-all-start.2) | async-done | bytes 1572896 | tf_op jit(solution)/shard_map/all_to_all | solution.py:248
  486.7 2.6 copy.347
  489.3 2.9 multiply_reduce_fusion.15
  494.1 2.6 copy.352
  496.8 3.5 reshape.799
  500.2 10.8 %gather_fusion = bf16[528,3072]{1,0:T(8,128)(2,1)} fusion(bf16[256,3072]{1,0:T(8,128)(2,1)} %reshape.799, s32[1024]{0:T(1024)S(1)} %pad_clamp_fusion.1), kind=kCustom, calls=%fused_computation | custom fusion | bytes 6490176 | tf_op jit(solution)/shard_map/jit(_take)/gather | solution.py:275
  511.0 3.8 gather.11
  514.9 2.6 select_multiply_fusion
  517.4 49.3 %all_to_all.53 = bf16[16,33,3072]{2,1,0:T(8,128)(2,1)} all-to-all(bf16[16,33,3072]{2,1,0:T(8,128)(2,1)S(1)} %select_multiply_fusion), channel_id=1, replica_groups=mesh['seq'=8,'exp'=16] {'exp'}, dimensions={0} | all-to-all | bytes 6488064 | tf_op jit(solution)/shard_map/all_to_all | solution.py:279
  566.7 3.9 reshape.800
  570.6 6.6 fusion.607
  580.9 4.6 fusion.41
  585.5 5.5 multiply_convert_fusion
  595.5 3.5 convolution_convert_fusion
  599.0 3.8 reshape.801
  602.9 6.8 all-to-all-start.4
  612.3 50.5 %all-to-all-done.4 = bf16[16,33,3072]{2,1,0:T(8,128)(2,1)} async-done(((bf16[16,33,3072]{2,1,0:T(8,128)(2,1)}), bf16[16,33,3072]{2,1,0:T(8,128)(2,1)}, u32[]{:S(2)}, u32[]{:S(2)}) %all-to-all-start.4) | async-done | bytes 3244064 | tf_op jit(solution)/shard_map/all_to_all | solution.py:298
  662.9 3.9 reshape.802
  666.7 9.4 %gather_fusion.1 = bf16[512,3072]{1,0:T(8,128)(2,1)} fusion(bf16[528,3072]{1,0:T(8,128)(2,1)} %reshape.802, s32[1024]{0:T(1024)S(1)} %pad_clamp_fusion), kind=kCustom, calls=%fused_computation.1 | custom fusion | bytes 6293504 | tf_op jit(solution)/shard_map/jit(_take)/gather | solution.py:310
  676.1 7.2 %reshape.814 = bf16[128,2,2,3072]{3,2,1,0:T(2,128)(2,1)} reshape(bf16[512,3072]{1,0:T(8,128)(2,1)} %gather_fusion.1) | data formatting | bytes 6291456 | tf_op jit(solution)/shard_map/jit(_take)/gather | solution.py:310
  683.3 6.6 fusion.81
  689.9 6.6 copy.356
  696.4 5.7 fusion.78
  702.1 2.6 copy.357
  (286 shorter events, 171.2 us)
Async XLA Ops:
  6.5 589.0 %copy-start = (bf16[1,512,3072]{2,1,0:T(8,128)(2,1)S(1)}, bf16[1,512,3072]{2,1,0:T(8,128)(2,1)}, u32[]{:S(2)}) copy-start(bf16[1,512,3072]{2,1,0:T(8,128)(2,1)} %param.23) | copy-start | bytes 9437188
  6.5 11.6 %copy-start.7 = (bf16[128,512]{1,0:T(8,128)(2,1)S(1)}, bf16[128,512]{1,0:T(8,128)(2,1)}, u32[]{:S(2)}) copy-start(bf16[128,512]{1,0:T(8,128)(2,1)} %param.14) | copy-start | bytes 393220
  6.5 11.7 %copy-start.8 = (bf16[128,512]{1,0:T(8,128)(2,1)S(1)}, bf16[128,512]{1,0:T(8,128)(2,1)}, u32[]{:S(2)}) copy-start(bf16[128,512]{1,0:T(8,128)(2,1)} %param.13) | copy-start | bytes 393220
  11.1 16.8 %all-to-all-start.1 = ((bf16[64,16,384]{2,0,1:T(8,128)(2,1)}), bf16[64,16,384]{2,0,1:T(8,128)(2,1)}, u32[]{:S(2)}, u32[]{:S(2)}) async-start(bf16[64,16,384]{2,0,1:T(8,128)(2,1)} %copy.306), calls=%async_computation.1 | async-start | bytes 1572864 | tf_op jit(solution)/shard_map/all_to_all | solution.py:144
  17.4 330.9 %all-gather.5.cloned.1.call-start = ((), (), s32[]{:S(2)}) async-start(), calls=%async_computation.6 | async-start | bytes 2654208 | tf_op jit(solution)/shard_map/all_gather | solution.py:227
  27.9 21.4 %all-to-all-start = ((bf16[128,16,256]{2,0,1:T(8,128)(2,1)}), bf16[128,16,256]{2,0,1:T(8,128)(2,1)}, u32[]{:S(2)}, u32[]{:S(2)}) async-start(bf16[128,16,256]{2,0,1:T(8,128)(2,1)} %pad_maximum_fusion.1), calls=%async_computation | async-start | bytes 2097152 | tf_op jit(solution)/shard_map/all_to_all | solution.py:21
  35.3 379.7 %all-gather.3.cloned.1.call-start = ((), (), s32[]{:S(2)}) async-start(), calls=%async_computation.5 | async-start | bytes 13369344 | tf_op jit(solution)/shard_map/all_gather | solution.py:231
  45.6 14.1 %collective-permute-start.3 = (bf16[512,3,128]{2,0,1:T(8,128)(2,1)}, bf16[512,3,128]{2,0,1:T(8,128)(2,1)}, u32[]{:S(2)}, u32[]{:S(2)}) collective-permute-start(bf16[512,3,128]{2,0,1:T(8,128)(2,1)} %copy.310), channel_id=1, source_target_pairs={{0,16},{16,0},{32,48},{48,32},{64,80},{80,64},{96,112},{112,96},{1... | collective-permute-start | bytes 1179656 | tf_op jit(solution)/shard_map/ppermute | solution.py:32
  50.5 17.3 %collective-permute-start = (bf16[1024,128]{1,0:T(8,128)(2,1)S(1)}, bf16[1024,128]{1,0:T(8,128)(2,1)S(1)}, u32[]{:S(2)}, u32[]{:S(2)}) collective-permute-start(bf16[1024,128]{1,0:T(8,128)(2,1)S(1)} %get-tuple-element.49), channel_id=1, source_target_pairs={{0,16},{16,0},{32,48},{48,32},{64,80},{80,64},{96,112},{112,96},{1... | collective-permute-start | bytes 786440 | tf_op jit(solution)/shard_map/ppermute | solution.py:32
  52.1 24.0 %collective-permute-start.6 = (bf16[1024,128]{1,0:T(8,128)(2,1)S(1)}, bf16[1024,128]{1,0:T(8,128)(2,1)S(1)}, u32[]{:S(2)}, u32[]{:S(2)}) collective-permute-start(bf16[1024,128]{1,0:T(8,128)(2,1)S(1)} %get-tuple-element.48), channel_id=1, source_target_pairs={{0,16},{16,0},{32,48},{48,32},{64,80},{80,64},{96,112},{112,96},{1... | collective-permute-start | bytes 786440 | tf_op jit(solution)/shard_map/ppermute | solution.py:32
  52.6 26.9 %collective-permute-start.9 = (bf16[1024,128]{1,0:T(8,128)(2,1)S(1)}, bf16[1024,128]{1,0:T(8,128)(2,1)S(1)}, u32[]{:S(2)}, u32[]{:S(2)}) collective-permute-start(bf16[1024,128]{1,0:T(8,128)(2,1)S(1)} %get-tuple-element.50), channel_id=1, source_target_pairs={{0,16},{16,32},{32,48},{48,64},{64,80},{80,96},{96,112},{112,0},{1... | collective-permute-start | bytes 786440 | tf_op jit(solution)/shard_map/ppermute | solution.py:38
  54.1 35.8 %copy-start.6 = (pred[512,1024]{0,1:T(8,128)(4,1)S(1)}, pred[512,1024]{0,1:T(8,128)(4,1)}, u32[]{:S(2)}) copy-start(pred[512,1024]{0,1:T(8,128)(4,1)} %broadcast_compare_fusion.1) | copy-start | bytes 1572868
  54.1 33.3 %collective-permute-start.11 = (bf16[1024,128]{1,0:T(8,128)(2,1)S(1)}, bf16[1024,128]{1,0:T(8,128)(2,1)S(1)}, u32[]{:S(2)}, u32[]{:S(2)}) collective-permute-start(bf16[1024,128]{1,0:T(8,128)(2,1)S(1)} %get-tuple-element.47), channel_id=1, source_target_pairs={{0,16},{16,32},{32,48},{48,64},{64,80},{80,96},{96,112},{112,0},{1... | collective-permute-start | bytes 786440 | tf_op jit(solution)/shard_map/ppermute | solution.py:38
  59.7 62.4 %collective-permute-start.4 = (bf16[512,3,128]{2,0,1:T(8,128)(2,1)}, bf16[512,3,128]{2,0,1:T(8,128)(2,1)S(1)}, u32[]{:S(2)}, u32[]{:S(2)}) collective-permute-start(bf16[512,3,128]{2,0,1:T(8,128)(2,1)} %collective-permute-done.3), channel_id=1, source_target_pairs={{0,32},{16,48},{32,0},{48,16},{64,96},{80,112},{96,64},{112,80},{1... | collective-permute-start | bytes 1179656 | tf_op jit(solution)/shard_map/ppermute | solution.py:32
  67.8 38.2 %collective-permute-start.1 = (bf16[1024,128]{1,0:T(8,128)(2,1)S(1)}, bf16[1024,128]{1,0:T(8,128)(2,1)S(1)}, u32[]{:S(2)}, u32[]{:S(2)}) collective-permute-start(bf16[1024,128]{1,0:T(8,128)(2,1)S(1)} %collective-permute-done), channel_id=1, source_target_pairs={{0,32},{16,48},{32,0},{48,16},{64,96},{80,112},{96,64},{112,80},{1... | collective-permute-start | bytes 786440 | tf_op jit(solution)/shard_map/ppermute | solution.py:32
  76.0 35.6 %collective-permute-start.7 = (bf16[1024,128]{1,0:T(8,128)(2,1)S(1)}, bf16[1024,128]{1,0:T(8,128)(2,1)S(1)}, u32[]{:S(2)}, u32[]{:S(2)}) collective-permute-start(bf16[1024,128]{1,0:T(8,128)(2,1)S(1)} %collective-permute-done.6), channel_id=1, source_target_pairs={{0,32},{16,48},{32,0},{48,16},{64,96},{80,112},{96,64},{112,80},{1... | collective-permute-start | bytes 786440 | tf_op jit(solution)/shard_map/ppermute | solution.py:32
  79.5 36.8 %collective-permute-start.13 = (bf16[1024,128]{1,0:T(8,128)(2,1)S(1)}, bf16[1024,128]{1,0:T(8,128)(2,1)S(1)}, u32[]{:S(2)}, u32[]{:S(2)}) collective-permute-start(bf16[1024,128]{1,0:T(8,128)(2,1)S(1)} %collective-permute-done.9), channel_id=1, source_target_pairs={{0,16},{16,32},{32,48},{48,64},{64,80},{80,96},{96,112},{112,0},{1... | collective-permute-start | bytes 786440 | tf_op jit(solution)/shard_map/ppermute | solution.py:38
  87.4 33.8 %collective-permute-start.15 = (bf16[1024,128]{1,0:T(8,128)(2,1)S(1)}, bf16[1024,128]{1,0:T(8,128)(2,1)S(1)}, u32[]{:S(2)}, u32[]{:S(2)}) collective-permute-start(bf16[1024,128]{1,0:T(8,128)(2,1)S(1)} %collective-permute-done.11), channel_id=1, source_target_pairs={{0,16},{16,32},{32,48},{48,64},{64,80},{80,96},{96,112},{112,0},{1... | collective-permute-start | bytes 786440 | tf_op jit(solution)/shard_map/ppermute | solution.py:38
  92.5 76.4 %copy-start.5 = (pred[512,1024]{0,1:T(8,128)(4,1)S(1)}, pred[512,1024]{0,1:T(8,128)(4,1)}, u32[]{:S(2)}) copy-start(pred[512,1024]{0,1:T(8,128)(4,1)} %broadcast_compare_fusion) | copy-start | bytes 1572868
  106.1 30.1 %collective-permute-start.2 = (bf16[1024,128]{1,0:T(8,128)(2,1)S(1)}, bf16[1024,128]{1,0:T(8,128)(2,1)S(1)}, u32[]{:S(2)}, u32[]{:S(2)}) collective-permute-start(bf16[1024,128]{1,0:T(8,128)(2,1)S(1)} %collective-permute-done.1), channel_id=1, source_target_pairs={{0,64},{16,80},{32,96},{48,112},{64,0},{80,16},{96,32},{112,48},{1... | collective-permute-start | bytes 786440 | tf_op jit(solution)/shard_map/ppermute | solution.py:32
  111.6 30.2 %collective-permute-start.8 = (bf16[1024,128]{1,0:T(8,128)(2,1)S(1)}, bf16[1024,128]{1,0:T(8,128)(2,1)S(1)}, u32[]{:S(2)}, u32[]{:S(2)}) collective-permute-start(bf16[1024,128]{1,0:T(8,128)(2,1)S(1)} %collective-permute-done.7), channel_id=1, source_target_pairs={{0,64},{16,80},{32,96},{48,112},{64,0},{80,16},{96,32},{112,48},{1... | collective-permute-start | bytes 786440 | tf_op jit(solution)/shard_map/ppermute | solution.py:32
  116.2 25.6 %collective-permute-start.17 = (bf16[1024,128]{1,0:T(8,128)(2,1)S(1)}, bf16[1024,128]{1,0:T(8,128)(2,1)S(1)}, u32[]{:S(2)}, u32[]{:S(2)}) collective-permute-start(bf16[1024,128]{1,0:T(8,128)(2,1)S(1)} %collective-permute-done.13), channel_id=1, source_target_pairs={{0,16},{16,32},{32,48},{48,64},{64,80},{80,96},{96,112},{112,0},{1... | collective-permute-start | bytes 786440 | tf_op jit(solution)/shard_map/ppermute | solution.py:38
  121.1 20.7 %collective-permute-start.19 = (bf16[1024,128]{1,0:T(8,128)(2,1)S(1)}, bf16[1024,128]{1,0:T(8,128)(2,1)S(1)}, u32[]{:S(2)}, u32[]{:S(2)}) collective-permute-start(bf16[1024,128]{1,0:T(8,128)(2,1)S(1)} %collective-permute-done.15), channel_id=1, source_target_pairs={{0,16},{16,32},{32,48},{48,64},{64,80},{80,96},{96,112},{112,0},{1... | collective-permute-start | bytes 786440 | tf_op jit(solution)/shard_map/ppermute | solution.py:38
  122.1 46.8 %collective-permute-start.5 = (bf16[512,3,128]{2,0,1:T(8,128)(2,1)S(1)}, bf16[512,3,128]{2,0,1:T(8,128)(2,1)S(1)}, u32[]{:S(2)}, u32[]{:S(2)}) collective-permute-start(bf16[512,3,128]{2,0,1:T(8,128)(2,1)S(1)} %collective-permute-done.4), channel_id=1, source_target_pairs={{0,64},{16,80},{32,96},{48,112},{64,0},{80,16},{96,32},{112,48},{1... | collective-permute-start | bytes 1179656 | tf_op jit(solution)/shard_map/ppermute | solution.py:32
  136.2 43.8 %collective-permute-start.10 = (bf16[1024,128]{1,0:T(8,128)(2,1)S(1)}, bf16[1024,128]{1,0:T(8,128)(2,1)S(1)}, u32[]{:S(2)}, u32[]{:S(2)}) collective-permute-start(bf16[1024,128]{1,0:T(8,128)(2,1)S(1)} %collective-permute-done.2), channel_id=1, source_target_pairs={{0,16},{16,32},{32,48},{48,64},{64,80},{80,96},{96,112},{112,0},{1... | collective-permute-start | bytes 786440 | tf_op jit(solution)/shard_map/ppermute | solution.py:38
  141.8 40.6 %collective-permute-start.12 = (bf16[1024,128]{1,0:T(8,128)(2,1)S(1)}, bf16[1024,128]{1,0:T(8,128)(2,1)S(1)}, u32[]{:S(2)}, u32[]{:S(2)}) collective-permute-start(bf16[1024,128]{1,0:T(8,128)(2,1)S(1)} %collective-permute-done.8), channel_id=1, source_target_pairs={{0,16},{16,32},{32,48},{48,64},{64,80},{80,96},{96,112},{112,0},{1... | collective-permute-start | bytes 786440 | tf_op jit(solution)/shard_map/ppermute | solution.py:38
  141.8 46.2 %collective-permute-start.21 = (bf16[1024,128]{1,0:T(8,128)(2,1)S(1)}, bf16[1024,128]{1,0:T(8,128)(2,1)S(1)}, u32[]{:S(2)}, u32[]{:S(2)}) collective-permute-start(bf16[1024,128]{1,0:T(8,128)(2,1)S(1)} %collective-permute-done.17), channel_id=1, source_target_pairs={{0,16},{16,32},{32,48},{48,64},{64,80},{80,96},{96,112},{112,0},{1... | collective-permute-start | bytes 786440 | tf_op jit(solution)/shard_map/ppermute | solution.py:38
  141.8 46.7 %collective-permute-start.23 = (bf16[1024,128]{1,0:T(8,128)(2,1)S(1)}, bf16[1024,128]{1,0:T(8,128)(2,1)S(1)}, u32[]{:S(2)}, u32[]{:S(2)}) collective-permute-start(bf16[1024,128]{1,0:T(8,128)(2,1)S(1)} %collective-permute-done.19), channel_id=1, source_target_pairs={{0,16},{16,32},{32,48},{48,64},{64,80},{80,96},{96,112},{112,0},{1... | collective-permute-start | bytes 786440 | tf_op jit(solution)/shard_map/ppermute | solution.py:38
  186.3 12.9 %collective-permute-start.14 = (bf16[1024,128]{1,0:T(8,128)(2,1)S(1)}, bf16[1024,128]{1,0:T(8,128)(2,1)S(1)}, u32[]{:S(2)}, u32[]{:S(2)}) collective-permute-start(bf16[1024,128]{1,0:T(8,128)(2,1)S(1)} %collective-permute-done.10), channel_id=1, source_target_pairs={{0,16},{16,32},{32,48},{48,64},{64,80},{80,96},{96,112},{112,0},{1... | collective-permute-start | bytes 786440 | tf_op jit(solution)/shard_map/ppermute | solution.py:38
  187.9 16.9 %collective-permute-start.16 = (bf16[1024,128]{1,0:T(8,128)(2,1)S(1)}, bf16[1024,128]{1,0:T(8,128)(2,1)S(1)}, u32[]{:S(2)}, u32[]{:S(2)}) collective-permute-start(bf16[1024,128]{1,0:T(8,128)(2,1)S(1)} %collective-permute-done.12), channel_id=1, source_target_pairs={{0,16},{16,32},{32,48},{48,64},{64,80},{80,96},{96,112},{112,0},{1... | collective-permute-start | bytes 786440 | tf_op jit(solution)/shard_map/ppermute | solution.py:38
  188.0 22.4 %collective-permute-start.25 = (bf16[1024,128]{1,0:T(8,128)(2,1)S(1)}, bf16[1024,128]{1,0:T(8,128)(2,1)S(1)}, u32[]{:S(2)}, u32[]{:S(2)}) collective-permute-start(bf16[1024,128]{1,0:T(8,128)(2,1)S(1)} %collective-permute-done.21), channel_id=1, source_target_pairs={{0,16},{16,32},{32,48},{48,64},{64,80},{80,96},{96,112},{112,0},{1... | collective-permute-start | bytes 786440 | tf_op jit(solution)/shard_map/ppermute | solution.py:38
  188.5 27.5 %collective-permute-start.27 = (bf16[1024,128]{1,0:T(8,128)(2,1)S(1)}, bf16[1024,128]{1,0:T(8,128)(2,1)S(1)}, u32[]{:S(2)}, u32[]{:S(2)}) collective-permute-start(bf16[1024,128]{1,0:T(8,128)(2,1)S(1)} %collective-permute-done.23), channel_id=1, source_target_pairs={{0,16},{16,32},{32,48},{48,64},{64,80},{80,96},{96,112},{112,0},{1... | collective-permute-start | bytes 786440 | tf_op jit(solution)/shard_map/ppermute | solution.py:38
  208.7 12.9 %collective-permute-start.18 = (bf16[1024,128]{1,0:T(8,128)(2,1)S(1)}, bf16[1024,128]{1,0:T(8,128)(2,1)S(1)}, u32[]{:S(2)}, u32[]{:S(2)}) collective-permute-start(bf16[1024,128]{1,0:T(8,128)(2,1)S(1)} %collective-permute-done.14), channel_id=1, source_target_pairs={{0,16},{16,32},{32,48},{48,64},{64,80},{80,96},{96,112},{112,0},{1... | collective-permute-start | bytes 786440 | tf_op jit(solution)/shard_map/ppermute | solution.py:38
  210.3 17.0 %collective-permute-start.20 = (bf16[1024,128]{1,0:T(8,128)(2,1)S(1)}, bf16[1024,128]{1,0:T(8,128)(2,1)S(1)}, u32[]{:S(2)}, u32[]{:S(2)}) collective-permute-start(bf16[1024,128]{1,0:T(8,128)(2,1)S(1)} %collective-permute-done.16), channel_id=1, source_target_pairs={{0,16},{16,32},{32,48},{48,64},{64,80},{80,96},{96,112},{112,0},{1... | collective-permute-start | bytes 786440 | tf_op jit(solution)/shard_map/ppermute | solution.py:38
  210.4 22.5 %collective-permute-start.29 = (bf16[1024,128]{1,0:T(8,128)(2,1)S(1)}, bf16[1024,128]{1,0:T(8,128)(2,1)S(1)}, u32[]{:S(2)}, u32[]{:S(2)}) collective-permute-start(bf16[1024,128]{1,0:T(8,128)(2,1)S(1)} %collective-permute-done.25), channel_id=1, source_target_pairs={{0,16},{16,32},{32,48},{48,64},{64,80},{80,96},{96,112},{112,0},{1... | collective-permute-start | bytes 786440 | tf_op jit(solution)/shard_map/ppermute | solution.py:38
  216.1 22.5 %collective-permute-start.31 = (bf16[1024,128]{1,0:T(8,128)(2,1)S(1)}, bf16[1024,128]{1,0:T(8,128)(2,1)S(1)}, u32[]{:S(2)}, u32[]{:S(2)}) collective-permute-start(bf16[1024,128]{1,0:T(8,128)(2,1)S(1)} %collective-permute-done.27), channel_id=1, source_target_pairs={{0,16},{16,32},{32,48},{48,64},{64,80},{80,96},{96,112},{112,0},{1... | collective-permute-start | bytes 786440 | tf_op jit(solution)/shard_map/ppermute | solution.py:38
  231.2 12.9 %collective-permute-start.22 = (bf16[1024,128]{1,0:T(8,128)(2,1)S(1)}, bf16[1024,128]{1,0:T(8,128)(2,1)S(1)}, u32[]{:S(2)}, u32[]{:S(2)}) collective-permute-start(bf16[1024,128]{1,0:T(8,128)(2,1)S(1)} %collective-permute-done.18), channel_id=1, source_target_pairs={{0,16},{16,32},{32,48},{48,64},{64,80},{80,96},{96,112},{112,0},{1... | collective-permute-start | bytes 786440 | tf_op jit(solution)/shard_map/ppermute | solution.py:38
  232.8 17.0 %collective-permute-start.24 = (bf16[1024,128]{1,0:T(8,128)(2,1)S(1)}, bf16[1024,128]{1,0:T(8,128)(2,1)S(1)}, u32[]{:S(2)}, u32[]{:S(2)}) collective-permute-start(bf16[1024,128]{1,0:T(8,128)(2,1)S(1)} %collective-permute-done.20), channel_id=1, source_target_pairs={{0,16},{16,32},{32,48},{48,64},{64,80},{80,96},{96,112},{112,0},{1... | collective-permute-start | bytes 786440 | tf_op jit(solution)/shard_map/ppermute | solution.py:38
  232.9 63.5 %collective-permute-start.33 = (bf16[1024,128]{1,0:T(8,128)(2,1)S(1)}, bf16[1024,128]{1,0:T(8,128)(2,1)S(1)}, u32[]{:S(2)}, u32[]{:S(2)}) collective-permute-start(bf16[1024,128]{1,0:T(8,128)(2,1)S(1)} %collective-permute-done.29), channel_id=1, source_target_pairs={{0,16},{16,32},{32,48},{48,64},{64,80},{80,96},{96,112},{112,0},{1... | collective-permute-start | bytes 786440 | tf_op jit(solution)/shard_map/ppermute | solution.py:38
  238.5 69.6 %collective-permute-start.35 = (bf16[1024,128]{1,0:T(8,128)(2,1)S(1)}, bf16[1024,128]{1,0:T(8,128)(2,1)S(1)}, u32[]{:S(2)}, u32[]{:S(2)}) collective-permute-start(bf16[1024,128]{1,0:T(8,128)(2,1)S(1)} %collective-permute-done.31), channel_id=1, source_target_pairs={{0,16},{16,32},{32,48},{48,64},{64,80},{80,96},{96,112},{112,0},{1... | collective-permute-start | bytes 786440 | tf_op jit(solution)/shard_map/ppermute | solution.py:38
  253.7 12.9 %collective-permute-start.26 = (bf16[1024,128]{1,0:T(8,128)(2,1)S(1)}, bf16[1024,128]{1,0:T(8,128)(2,1)S(1)}, u32[]{:S(2)}, u32[]{:S(2)}) collective-permute-start(bf16[1024,128]{1,0:T(8,128)(2,1)S(1)} %collective-permute-done.22), channel_id=1, source_target_pairs={{0,16},{16,32},{32,48},{48,64},{64,80},{80,96},{96,112},{112,0},{1... | collective-permute-start | bytes 786440 | tf_op jit(solution)/shard_map/ppermute | solution.py:38
  255.3 15.4 %collective-permute-start.28 = (bf16[1024,128]{1,0:T(8,128)(2,1)S(1)}, bf16[1024,128]{1,0:T(8,128)(2,1)S(1)}, u32[]{:S(2)}, u32[]{:S(2)}) collective-permute-start(bf16[1024,128]{1,0:T(8,128)(2,1)S(1)} %collective-permute-done.24), channel_id=1, source_target_pairs={{0,16},{16,32},{32,48},{48,64},{64,80},{80,96},{96,112},{112,0},{1... | collective-permute-start | bytes 786440 | tf_op jit(solution)/shard_map/ppermute | solution.py:38
  274.6 12.9 %collective-permute-start.30 = (bf16[1024,128]{1,0:T(8,128)(2,1)S(1)}, bf16[1024,128]{1,0:T(8,128)(2,1)S(1)}, u32[]{:S(2)}, u32[]{:S(2)}) collective-permute-start(bf16[1024,128]{1,0:T(8,128)(2,1)S(1)} %collective-permute-done.26), channel_id=1, source_target_pairs={{0,16},{16,32},{32,48},{48,64},{64,80},{80,96},{96,112},{112,0},{1... | collective-permute-start | bytes 786440 | tf_op jit(solution)/shard_map/ppermute | solution.py:38
  276.2 14.5 %collective-permute-start.32 = (bf16[1024,128]{1,0:T(8,128)(2,1)S(1)}, bf16[1024,128]{1,0:T(8,128)(2,1)S(1)}, u32[]{:S(2)}, u32[]{:S(2)}) collective-permute-start(bf16[1024,128]{1,0:T(8,128)(2,1)S(1)} %collective-permute-done.28), channel_id=1, source_target_pairs={{0,16},{16,32},{32,48},{48,64},{64,80},{80,96},{96,112},{112,0},{1... | collective-permute-start | bytes 786440 | tf_op jit(solution)/shard_map/ppermute | solution.py:38
  294.6 12.4 %collective-permute-start.34 = (bf16[1024,128]{1,0:T(8,128)(2,1)S(1)}, bf16[1024,128]{1,0:T(8,128)(2,1)S(1)}, u32[]{:S(2)}, u32[]{:S(2)}) collective-permute-start(bf16[1024,128]{1,0:T(8,128)(2,1)S(1)} %collective-permute-done.30), channel_id=1, source_target_pairs={{0,16},{16,32},{32,48},{48,64},{64,80},{80,96},{96,112},{112,0},{1... | collective-permute-start | bytes 786440 | tf_op jit(solution)/shard_map/ppermute | solution.py:38
  296.2 13.6 %collective-permute-start.36 = (bf16[1024,128]{1,0:T(8,128)(2,1)S(1)}, bf16[1024,128]{1,0:T(8,128)(2,1)S(1)}, u32[]{:S(2)}, u32[]{:S(2)}) collective-permute-start(bf16[1024,128]{1,0:T(8,128)(2,1)S(1)} %collective-permute-done.32), channel_id=1, source_target_pairs={{0,16},{16,32},{32,48},{48,64},{64,80},{80,96},{96,112},{112,0},{1... | collective-permute-start | bytes 786440 | tf_op jit(solution)/shard_map/ppermute | solution.py:38
  316.7 30.2 %copy-start.11 = (s32[128,2]{0,1:T(2,128)S(1)}, s32[128,2]{0,1:T(2,128)}, u32[]{:S(2)}) copy-start(s32[128,2]{0,1:T(2,128)} %param.19) | copy-start | bytes 3076
  316.8 10.5 %collective-permute-start.37 = (bf16[512,384]{0,1:T(8,128)(2,1)S(1)}, bf16[512,384]{0,1:T(8,128)(2,1)S(1)}, u32[]{:S(2)}, u32[]{:S(2)}) collective-permute-start(bf16[512,384]{0,1:T(8,128)(2,1)S(1)} %fusion.302), channel_id=1, source_target_pairs={{0,16},{16,0},{32,48},{48,32},{64,80},{80,64},{96,112},{112,96},{1... | collective-permute-start | bytes 1179656 | tf_op jit(solution)/shard_map/ppermute | solution.py:32
  327.3 9.3 %collective-permute-start.38 = (bf16[512,384]{0,1:T(8,128)(2,1)S(1)}, bf16[512,384]{0,1:T(8,128)(2,1)S(1)}, u32[]{:S(2)}, u32[]{:S(2)}) collective-permute-start(bf16[512,384]{0,1:T(8,128)(2,1)S(1)} %collective-permute-done.37), channel_id=1, source_target_pairs={{0,32},{16,48},{32,0},{48,16},{64,96},{80,112},{96,64},{112,80},{1... | collective-permute-start | bytes 1179656 | tf_op jit(solution)/shard_map/ppermute | solution.py:32
  336.6 9.3 %collective-permute-start.39 = (bf16[512,384]{0,1:T(8,128)(2,1)S(1)}, bf16[512,384]{0,1:T(8,128)(2,1)S(1)}, u32[]{:S(2)}, u32[]{:S(2)}) collective-permute-start(bf16[512,384]{0,1:T(8,128)(2,1)S(1)} %collective-permute-done.38), channel_id=1, source_target_pairs={{0,64},{16,80},{32,96},{48,112},{64,0},{80,16},{96,32},{112,48},{1... | collective-permute-start | bytes 1179656 | tf_op jit(solution)/shard_map/ppermute | solution.py:32
  415.0 3.4 copy-start.4
  417.1 5.5 copy-start.3
  458.2 7.3 %copy-start.10 = (bf16[6144]{0:T(1024)(128)(2,1)S(1)}, bf16[6144]{0:T(1024)(128)(2,1)}, u32[]{:S(2)}) copy-start(bf16[6144]{0:T(1024)(128)(2,1)} %param.17) | copy-start | bytes 36868
  459.7 26.9 %all-to-all-start.2 = ((bf16[16,128,384]{2,1,0:T(8,128)(2,1)}), bf16[16,128,384]{2,1,0:T(8,128)(2,1)}, u32[]{:S(2)}, u32[]{:S(2)}) async-start(bf16[16,128,384]{2,1,0:T(8,128)(2,1)} %copy.346), calls=%async_computation.2 | async-start | bytes 3145728 | tf_op jit(solution)/shard_map/all_to_all | solution.py:248
  489.3 2.9 copy-start.1
  489.3 2.9 copy-start.2
  577.2 3.3 collective-permute-start.40
  585.5 5.5 copy-start.12
  593.5 2.0 collective-permute-start.41
  602.9 7.7 %copy-start.9 = (bf16[6144,8]{0,1:T(8,128)(2,1)S(1)}, bf16[6144,8]{0,1:T(8,128)(2,1)}, u32[]{:S(2)}) copy-start(bf16[6144,8]{0,1:T(8,128)(2,1)} %param.18) | copy-start | bytes 294916
  602.9 60.0 %all-to-all-start.4 = ((bf16[16,33,3072]{2,1,0:T(8,128)(2,1)}), bf16[16,33,3072]{2,1,0:T(8,128)(2,1)}, u32[]{:S(2)}, u32[]{:S(2)}) async-start(bf16[16,33,3072]{2,1,0:T(8,128)(2,1)} %reshape.801), calls=%async_computation.4 | async-start | bytes 7864320 | tf_op jit(solution)/shard_map/all_to_all | solution.py:298
Sparse Core Ops, SparseCore 0:
  20.5 90.7 all-gather.4
  347.0 67.9 all-gather.2
where the time goes:
time: 721 us; the launch traced here: 712 us
  waiting for transfers between devices  322 us (45%)
  matrix products  87 us (12%)
  local copies, waits for them, and re-layouts  83.5 us (12%)
  other arithmetic  77.6 us (11%)
  starting transfers between devices  76.9 us (11%)
  blocking collectives  49.3 us (7%)
  between operations  15.1 us (2%)
    ppermute x14, waiting for transfers between devices, swapped(): lax.ppermute(x, axis, [(i, i ^ 1 << distance) for i in range(lax.axis_siz...  98.9 us
    ppermute x28, waiting for transfers between devices, passed_along(): return lax.ppermute(value, axis, pairs)  79.1 us
    all_gather x1, waiting for transfers between devices, per_device(): shard_piece = lax.all_gather(attended, 'exp', axis=0, tiled=True)  66.8 us
    all_to_all x1, waiting for transfers between devices, per_device(): lax.all_to_all(expert_out.reshape(exp_count, CAP, piece_width), 'exp', sp...  50.5 us
    all_to_all x1, blocking collectives, per_device(): lax.all_to_all(send_rows, 'exp', split_axis=0, concat_axis=0, tiled=True)  49.3 us
    dot_general x17, matrix products, attend(): jnp.einsum('qhk,kd->qhd', exp_terms.astype(jnp.bfloat16), value_rows, pre...  27 us
    dynamic_update_slice x15, other arithmetic, per_device(): carried = lax.dynamic_update_slice(carried, present + product, corner)  26.5 us
    ppermute x14, starting transfers between devices, swapped(): lax.ppermute(x, axis, [(i, i ^ 1 << distance) for i in range(lax.axis_siz...  26 us
  transfers between devices with their start and end apart: 48, of which 35 were waited for; matrix products, arithmetic and copies ran while one was open for 13% of the time, Pallas kernels for 0%

commit v1 on v0

--- a/solution.py
+++ b/solution.py
@@ -228,7 +228,10 @@
     column_count = weight_rows.shape[1]
     blank_sum = jnp.zeros((exp_count, token_rows, split_count, column_count), jnp.float32)
     carried = blank_sum
-    shard_piece = lax.all_gather(attended, "exp", axis=0, tiled=True)
+    n_dev = lax.axis_size("exp")
+    blocks = jnp.stack([attended for _ in range(n_dev)])
+    blocks = lax.all_to_all(blocks, "exp", split_axis=0, concat_axis=0)
+    shard_piece = jnp.concatenate(blocks, axis=0)
     start_row = jnp.int32(0)
     shard_total = shard_piece.shape[0] // query_count
     for shard_index in range(shard_total):

time: 721 us -> 813 us (1.13)
  waiting for transfers between devices: 322 us -> 393 us
  other arithmetic: 77.6 us -> 50.9 us
  local copies, waits for them, and re-layouts: 83.5 us -> 103 us
  starting transfers between devices: 76.9 us -> 92.8 us
  matrix products: 87 us -> 99.6 us
    all_to_all x0 -> x1, waiting for transfers between devices: none -> 168 us  [per_device(): blocks = lax.all_to_all(blocks, 'exp', split_axis=0, concat_axis=0)]
    all_gather x1 -> x0, waiting for transfers between devices: 66.8 us -> none  [per_device(): shard_piece = lax.all_gather(attended, 'exp', axis=0, tiled=True)]
    dynamic_update_slice x15 -> x0, other arithmetic: 26.5 us -> none  [per_device(): carried = lax.dynamic_update_slice(carried, present + product, corner)]
    ppermute x14, waiting for transfers between devices: 98.9 us -> 81.8 us  [swapped(): lax.ppermute(x, axis, [(i, i ^ 1 << distance) for i in range(lax.axis_siz...]
    ppermute x28, waiting for transfers between devices: 79.1 us -> 66 us  [passed_along(): return lax.ppermute(value, axis, pairs)]
    dot_general x16, matrix products: 14.7 us -> 27.1 us  [per_device(): jnp.dot(rows_now, weight_slice, preferred_element_type=jnp.float32)]
    slice x1 -> x2, local copies, waits for them, and re-layouts: 0.21 us -> 9.95 us  [the longest x1 9.74 us: per_device(): shard_piece[shard_index * query_count:(shard_index + 1) * query_count]]
  transfers between devices with their start and end apart: 48 -> 48, of which waited for: 35 -> 36; matrix products, arithmetic and copies ran while one was open for 13% -> 12% of each run, Pallas kernels for 0% -> 0%
where the time goes in v1:
time: 813 us; the launch traced here: 803 us
  waiting for transfers between devices  393 us (48%)
  local copies, waits for them, and re-layouts  103 us (13%)
  matrix products  99.6 us (12%)
  starting transfers between devices  92.8 us (11%)
  other arithmetic  50.9 us (6%)
  blocking collectives  49 us (6%)
  between operations  15.5 us (2%)
    all_to_all x1, waiting for transfers between devices, per_device(): blocks = lax.all_to_all(blocks, 'exp', split_axis=0, concat_axis=0)  168 us
    ppermute x14, waiting for transfers between devices, swapped(): lax.ppermute(x, axis, [(i, i ^ 1 << distance) for i in range(lax.axis_siz...  81.8 us
    ppermute x28, waiting for transfers between devices, passed_along(): return lax.ppermute(value, axis, pairs)  66 us
    all_to_all x1, waiting for transfers between devices, per_device(): lax.all_to_all(expert_out.reshape(exp_count, CAP, piece_width), 'exp', sp...  50.5 us
    all_to_all x1, blocking collectives, per_device(): lax.all_to_all(send_rows, 'exp', split_axis=0, concat_axis=0, tiled=True)  49 us
    ppermute x14, starting transfers between devices, swapped(): lax.ppermute(x, axis, [(i, i ^ 1 << distance) for i in range(lax.axis_siz...  31.8 us
    ppermute x28, starting transfers between devices, passed_along(): return lax.ppermute(value, axis, pairs)  30.3 us
    dot_general x17, matrix products, attend(): jnp.einsum('qhk,kd->qhd', exp_terms.astype(jnp.bfloat16), value_rows, pre...  27.2 us
  transfers between devices with their start and end apart: 48, of which 36 were waited for; matrix products, arithmetic and copies ran while one was open for 12% of the time, Pallas kernels for 0%

profile of v1, /device:TPU:8, one launch (start us, length us, event | category | flops | bytes accessed | tf_op | source)
XLA Modules:
  0.0 803.2 jit_solution(15779343162226646467)
XLA Ops:
  11.1 6.3 all-to-all-start.1
  18.8 9.1 %all-to-all-done.1 = bf16[64,16,384]{2,0,1:T(8,128)(2,1)} async-done(((bf16[64,16,384]{2,0,1:T(8,128)(2,1)}), bf16[64,16,384]{2,0,1:T(8,128)(2,1)}, u32[]{:S(2)}, u32[]{:S(2)}) %all-to-all-start.1) | async-done | bytes 786464 | tf_op jit(solution)/shard_map/all_to_all | solution.py:144
  27.9 7.4 all-to-all-start
  57.8 4.7 collective-permute-start.4
  63.4 3.0 collective-permute-start.1
  66.4 2.6 collective-permute-done.6
  69.0 3.0 collective-permute-start.7
  76.1 3.1 collective-permute-done.11
  81.7 2.7 fusion.257
  84.4 12.2 %collective-permute-done.1 = bf16[1024,128]{1,0:T(8,128)(2,1)S(1)} collective-permute-done((bf16[1024,128]{1,0:T(8,128)(2,1)S(1)}, bf16[1024,128]{1,0:T(8,128)(2,1)S(1)}, u32[]{:S(2)}, u32[]{:S(2)}) %collective-permute-start.1) | collective-permute-done | bytes 262176 | tf_op jit(solution)/shard_map/ppermute | solution.py:32
  96.6 3.6 collective-permute-start.2
  102.1 3.6 collective-permute-start.8
  107.0 3.6 collective-permute-done.15
  112.7 3.8 collective-permute-start.5
  117.8 7.9 collective-permute-done.2
  125.7 19.7 %collective-permute-done.8 = bf16[1024,128]{1,0:T(8,128)(2,1)S(1)} collective-permute-done((bf16[1024,128]{1,0:T(8,128)(2,1)S(1)}, bf16[1024,128]{1,0:T(8,128)(2,1)S(1)}, u32[]{:S(2)}, u32[]{:S(2)}) %collective-permute-start.8) | collective-permute-done | bytes 262176 | tf_op jit(solution)/shard_map/ppermute | solution.py:32
  145.4 6.5 collective-permute-done.5
  173.0 6.4 collective-permute-start.27
  179.5 3.0 collective-permute-done.14
  184.9 3.2 collective-permute-done.16
  195.6 3.7 collective-permute-done.27
  199.3 2.6 collective-permute-start.31
  201.9 3.0 collective-permute-done.18
  207.4 3.2 collective-permute-done.20
  218.1 3.7 collective-permute-done.31
  221.8 2.6 collective-permute-start.35
  224.4 3.0 collective-permute-done.22
  229.9 3.2 collective-permute-done.24
  239.1 10.8 %collective-permute-done.26 = bf16[1024,128]{1,0:T(8,128)(2,1)S(1)} collective-permute-done((bf16[1024,128]{1,0:T(8,128)(2,1)S(1)}, bf16[1024,128]{1,0:T(8,128)(2,1)S(1)}, u32[]{:S(2)}, u32[]{:S(2)}) %collective-permute-start.26) | collective-permute-done | bytes 262176 | tf_op jit(solution)/shard_map/ppermute | solution.py:38
  258.6 10.3 %collective-permute-done.30 = bf16[1024,128]{1,0:T(8,128)(2,1)S(1)} collective-permute-done((bf16[1024,128]{1,0:T(8,128)(2,1)S(1)}, bf16[1024,128]{1,0:T(8,128)(2,1)S(1)}, u32[]{:S(2)}, u32[]{:S(2)}) %collective-permute-start.30) | collective-permute-done | bytes 262176 | tf_op jit(solution)/shard_map/ppermute | solution.py:38
  277.6 9.4 %collective-permute-done.34 = bf16[1024,128]{1,0:T(8,128)(2,1)S(1)} collective-permute-done((bf16[1024,128]{1,0:T(8,128)(2,1)S(1)}, bf16[1024,128]{1,0:T(8,128)(2,1)S(1)}, u32[]{:S(2)}, u32[]{:S(2)}) %collective-permute-start.34) | collective-permute-done | bytes 262176 | tf_op jit(solution)/shard_map/ppermute | solution.py:38
  295.5 11.1 %collective-permute-done.37 = bf16[512,384]{0,1:T(8,128)(2,1)S(1)} collective-permute-done((bf16[512,384]{0,1:T(8,128)(2,1)S(1)}, bf16[512,384]{0,1:T(8,128)(2,1)S(1)}, u32[]{:S(2)}, u32[]{:S(2)}) %collective-permute-start.37) | collective-permute-done | bytes 393248 | tf_op jit(solution)/shard_map/ppermute | solution.py:32
  306.7 9.3 %collective-permute-done.38 = bf16[512,384]{0,1:T(8,128)(2,1)S(1)} collective-permute-done((bf16[512,384]{0,1:T(8,128)(2,1)S(1)}, bf16[512,384]{0,1:T(8,128)(2,1)S(1)}, u32[]{:S(2)}, u32[]{:S(2)}) %collective-permute-start.38) | collective-permute-done | bytes 393248 | tf_op jit(solution)/shard_map/ppermute | solution.py:32
  316.0 4.8 collective-permute-start.39
  320.8 5.7 collective-permute-done.39
  329.8 7.3 stack.11
  337.1 5.7 all-to-all-start.2
  344.6 167.6 %all-to-all-done.2 = bf16[16,1024,384]{2,1,0:T(8,128)(2,1)} async-done(((bf16[16,1024,384]{2,1,0:T(8,128)(2,1)}), bf16[16,1024,384]{2,1,0:T(8,128)(2,1)}, u32[]{:S(2)}, u32[]{:S(2)}) %all-to-all-start.2) | async-done | bytes 12582944 | tf_op jit(solution)/shard_map/all_to_all | solution.py:233
  512.1 9.7 %fusion.551 = (bf16[1,1024,384]{2,1,0:T(8,128)(2,1)}, bf16[1,1024,384]{2,1,0:T(8,128)(2,1)}, bf16[1,1024,384]{2,1,0:T(8,128)(2,1)}, bf16[1,1024,384]{2,1,0:T(8,1...) fusion(bf16[16,1024,384]{2,1,0:T(8,128)(2,1)} %all-to-all-done.2), kind=kLoop, calls=%fused_computation.725 | loop fusion | bytes 25165824 | tf_op jit(solution)/shard_map/slice | solution.py:242
  552.4 4.5 all-to-all-start.3
  557.2 2.6 copy.229
  561.5 16.6 %all-to-all-done.3 = bf16[16,128,384]{2,1,0:T(8,128)(2,1)} async-done(((bf16[16,128,384]{2,1,0:T(8,128)(2,1)}), bf16[16,128,384]{2,1,0:T(8,128)(2,1)}, u32[]{:S(2)}, u32[]{:S(2)}) %all-to-all-start.3) | async-done | bytes 1572896 | tf_op jit(solution)/shard_map/all_to_all | solution.py:251
  578.1 2.6 copy.258
  580.7 2.9 multiply_reduce_fusion.15
  585.5 2.6 copy.263
  588.1 3.5 reshape.773
  591.6 10.8 %gather_fusion = bf16[528,3072]{1,0:T(8,128)(2,1)} fusion(bf16[256,3072]{1,0:T(8,128)(2,1)} %reshape.773, s32[1024]{0:T(1024)S(1)} %pad_clamp_fusion.1), kind=kCustom, calls=%fused_computation | custom fusion | bytes 6490176 | tf_op jit(solution)/shard_map/jit(_take)/gather | solution.py:278
  602.4 3.8 gather.11
  608.8 49.0 %all_to_all.58 = bf16[16,33,3072]{2,1,0:T(8,128)(2,1)} all-to-all(bf16[16,33,3072]{2,1,0:T(8,128)(2,1)S(1)} %select_multiply_fusion), channel_id=1, replica_groups=mesh['seq'=8,'exp'=16] {'exp'}, dimensions={0} | all-to-all | bytes 6488064 | tf_op jit(solution)/shard_map/all_to_all | solution.py:282
  657.8 3.9 reshape.774
  661.6 6.6 fusion.554
  672.1 4.6 fusion.41
  676.8 5.5 multiply_convert_fusion
  686.7 3.5 convolution_convert_fusion
  690.2 3.8 reshape.775
  694.1 6.9 all-to-all-start.5
  703.6 50.5 %all-to-all-done.5 = bf16[16,33,3072]{2,1,0:T(8,128)(2,1)} async-done(((bf16[16,33,3072]{2,1,0:T(8,128)(2,1)}), bf16[16,33,3072]{2,1,0:T(8,128)(2,1)}, u32[]{:S(2)}, u32[]{:S(2)}) %all-to-all-start.5) | async-done | bytes 3244064 | tf_op jit(solution)/shard_map/all_to_all | solution.py:301
  754.1 3.9 reshape.776
  758.0 9.4 %gather_fusion.1 = bf16[512,3072]{1,0:T(8,128)(2,1)} fusion(bf16[528,3072]{1,0:T(8,128)(2,1)} %reshape.776, s32[1024]{0:T(1024)S(1)} %pad_clamp_fusion), kind=kCustom, calls=%fused_computation.1 | custom fusion | bytes 6293504 | tf_op jit(solution)/shard_map/jit(_take)/gather | solution.py:313
  767.4 7.2 reshape.788
  774.6 6.5 fusion.81
  781.1 6.6 copy.267
  787.7 5.7 fusion.78
  793.4 2.6 copy.268
  (298 shorter events, 170.0 us)
Async XLA Ops:
  6.5 680.2 %copy-start = (bf16[1,512,3072]{2,1,0:T(8,128)(2,1)S(1)}, bf16[1,512,3072]{2,1,0:T(8,128)(2,1)}, u32[]{:S(2)}) copy-start(bf16[1,512,3072]{2,1,0:T(8,128)(2,1)} %param.23) | copy-start | bytes 9437188
  6.5 10.9 %copy-start.20 = (bf16[128,512]{1,0:T(8,128)(2,1)S(1)}, bf16[128,512]{1,0:T(8,128)(2,1)}, u32[]{:S(2)}) copy-start(bf16[128,512]{1,0:T(8,128)(2,1)} %param.14) | copy-start | bytes 393220
  6.5 10.9 %copy-start.21 = (bf16[128,512]{1,0:T(8,128)(2,1)S(1)}, bf16[128,512]{1,0:T(8,128)(2,1)}, u32[]{:S(2)}) copy-start(bf16[128,512]{1,0:T(8,128)(2,1)} %param.13) | copy-start | bytes 393220
  11.1 16.8 %all-to-all-start.1 = ((bf16[64,16,384]{2,0,1:T(8,128)(2,1)}), bf16[64,16,384]{2,0,1:T(8,128)(2,1)}, u32[]{:S(2)}, u32[]{:S(2)}) async-start(bf16[64,16,384]{2,0,1:T(8,128)(2,1)} %copy.232), calls=%async_computation.1 | async-start | bytes 1572864 | tf_op jit(solution)/shard_map/all_to_all | solution.py:144
  27.9 20.9 %all-to-all-start = ((bf16[128,16,256]{2,0,1:T(8,128)(2,1)}), bf16[128,16,256]{2,0,1:T(8,128)(2,1)}, u32[]{:S(2)}, u32[]{:S(2)}) async-start(bf16[128,16,256]{2,0,1:T(8,128)(2,1)} %pad_maximum_fusion.1), calls=%async_computation | async-start | bytes 2097152 | tf_op jit(solution)/shard_map/all_to_all | solution.py:21
  45.5 12.3 %collective-permute-start.3 = (bf16[512,3,128]{2,0,1:T(8,128)(2,1)}, bf16[512,3,128]{2,0,1:T(8,128)(2,1)}, u32[]{:S(2)}, u32[]{:S(2)}) collective-permute-start(bf16[512,3,128]{2,0,1:T(8,128)(2,1)} %copy.236), channel_id=1, source_target_pairs={{0,16},{16,0},{32,48},{48,32},{64,80},{80,64},{96,112},{112,96},{1... | collective-permute-start | bytes 1179656 | tf_op jit(solution)/shard_map/ppermute | solution.py:32
  50.0 31.7 %copy-start.19 = (pred[512,1024]{0,1:T(8,128)(4,1)S(1)}, pred[512,1024]{0,1:T(8,128)(4,1)}, u32[]{:S(2)}) copy-start(pred[512,1024]{0,1:T(8,128)(4,1)} %broadcast_compare_fusion.1) | copy-start | bytes 1572868
  50.0 13.3 %collective-permute-start = (bf16[1024,128]{1,0:T(8,128)(2,1)S(1)}, bf16[1024,128]{1,0:T(8,128)(2,1)S(1)}, u32[]{:S(2)}, u32[]{:S(2)}) collective-permute-start(bf16[1024,128]{1,0:T(8,128)(2,1)S(1)} %get-tuple-element.57), channel_id=1, source_target_pairs={{0,16},{16,0},{32,48},{48,32},{64,80},{80,64},{96,112},{112,96},{1... | collective-permute-start | bytes 786440 | tf_op jit(solution)/shard_map/ppermute | solution.py:32
  51.6 17.4 %collective-permute-start.6 = (bf16[1024,128]{1,0:T(8,128)(2,1)S(1)}, bf16[1024,128]{1,0:T(8,128)(2,1)S(1)}, u32[]{:S(2)}, u32[]{:S(2)}) collective-permute-start(bf16[1024,128]{1,0:T(8,128)(2,1)S(1)} %get-tuple-element.56), channel_id=1, source_target_pairs={{0,16},{16,0},{32,48},{48,32},{64,80},{80,64},{96,112},{112,96},{1... | collective-permute-start | bytes 786440 | tf_op jit(solution)/shard_map/ppermute | solution.py:32
  52.1 21.5 %collective-permute-start.9 = (bf16[1024,128]{1,0:T(8,128)(2,1)S(1)}, bf16[1024,128]{1,0:T(8,128)(2,1)S(1)}, u32[]{:S(2)}, u32[]{:S(2)}) collective-permute-start(bf16[1024,128]{1,0:T(8,128)(2,1)S(1)} %get-tuple-element.58), channel_id=1, source_target_pairs={{0,16},{16,32},{32,48},{48,64},{64,80},{80,96},{96,112},{112,0},{1... | collective-permute-start | bytes 786440 | tf_op jit(solution)/shard_map/ppermute | solution.py:38
  53.6 25.6 %collective-permute-start.11 = (bf16[1024,128]{1,0:T(8,128)(2,1)S(1)}, bf16[1024,128]{1,0:T(8,128)(2,1)S(1)}, u32[]{:S(2)}, u32[]{:S(2)}) collective-permute-start(bf16[1024,128]{1,0:T(8,128)(2,1)S(1)} %get-tuple-element.55), channel_id=1, source_target_pairs={{0,16},{16,32},{32,48},{48,64},{64,80},{80,96},{96,112},{112,0},{1... | collective-permute-start | bytes 786440 | tf_op jit(solution)/shard_map/ppermute | solution.py:38
  57.8 54.8 %collective-permute-start.4 = (bf16[512,3,128]{2,0,1:T(8,128)(2,1)}, bf16[512,3,128]{2,0,1:T(8,128)(2,1)S(1)}, u32[]{:S(2)}, u32[]{:S(2)}) collective-permute-start(bf16[512,3,128]{2,0,1:T(8,128)(2,1)} %collective-permute-done.3), channel_id=1, source_target_pairs={{0,32},{16,48},{32,0},{48,16},{64,96},{80,112},{96,64},{112,80},{1... | collective-permute-start | bytes 1179656 | tf_op jit(solution)/shard_map/ppermute | solution.py:32
  63.4 33.2 %collective-permute-start.1 = (bf16[1024,128]{1,0:T(8,128)(2,1)S(1)}, bf16[1024,128]{1,0:T(8,128)(2,1)S(1)}, u32[]{:S(2)}, u32[]{:S(2)}) collective-permute-start(bf16[1024,128]{1,0:T(8,128)(2,1)S(1)} %collective-permute-done), channel_id=1, source_target_pairs={{0,32},{16,48},{32,0},{48,16},{64,96},{80,112},{96,64},{112,80},{1... | collective-permute-start | bytes 786440 | tf_op jit(solution)/shard_map/ppermute | solution.py:32
  69.0 33.1 %collective-permute-start.7 = (bf16[1024,128]{1,0:T(8,128)(2,1)S(1)}, bf16[1024,128]{1,0:T(8,128)(2,1)S(1)}, u32[]{:S(2)}, u32[]{:S(2)}) collective-permute-start(bf16[1024,128]{1,0:T(8,128)(2,1)S(1)} %collective-permute-done.6), channel_id=1, source_target_pairs={{0,32},{16,48},{32,0},{48,16},{64,96},{80,112},{96,64},{112,80},{1... | collective-permute-start | bytes 786440 | tf_op jit(solution)/shard_map/ppermute | solution.py:32
  73.6 32.2 %collective-permute-start.13 = (bf16[1024,128]{1,0:T(8,128)(2,1)S(1)}, bf16[1024,128]{1,0:T(8,128)(2,1)S(1)}, u32[]{:S(2)}, u32[]{:S(2)}) collective-permute-start(bf16[1024,128]{1,0:T(8,128)(2,1)S(1)} %collective-permute-done.9), channel_id=1, source_target_pairs={{0,16},{16,32},{32,48},{48,64},{64,80},{80,96},{96,112},{112,0},{1... | collective-permute-start | bytes 786440 | tf_op jit(solution)/shard_map/ppermute | solution.py:38
  79.2 31.4 %collective-permute-start.15 = (bf16[1024,128]{1,0:T(8,128)(2,1)S(1)}, bf16[1024,128]{1,0:T(8,128)(2,1)S(1)}, u32[]{:S(2)}, u32[]{:S(2)}) collective-permute-start(bf16[1024,128]{1,0:T(8,128)(2,1)S(1)} %collective-permute-done.11), channel_id=1, source_target_pairs={{0,16},{16,32},{32,48},{48,64},{64,80},{80,96},{96,112},{112,0},{1... | collective-permute-start | bytes 786440 | tf_op jit(solution)/shard_map/ppermute | solution.py:38
  84.4 67.6 %copy-start.3 = (pred[512,1024]{0,1:T(8,128)(4,1)S(1)}, pred[512,1024]{0,1:T(8,128)(4,1)}, u32[]{:S(2)}) copy-start(pred[512,1024]{0,1:T(8,128)(4,1)} %broadcast_compare_fusion) | copy-start | bytes 1572868
  96.6 29.1 %collective-permute-start.2 = (bf16[1024,128]{1,0:T(8,128)(2,1)S(1)}, bf16[1024,128]{1,0:T(8,128)(2,1)S(1)}, u32[]{:S(2)}, u32[]{:S(2)}) collective-permute-start(bf16[1024,128]{1,0:T(8,128)(2,1)S(1)} %collective-permute-done.1), channel_id=1, source_target_pairs={{0,64},{16,80},{32,96},{48,112},{64,0},{80,16},{96,32},{112,48},{1... | collective-permute-start | bytes 786440 | tf_op jit(solution)/shard_map/ppermute | solution.py:32
  102.1 43.2 %collective-permute-start.8 = (bf16[1024,128]{1,0:T(8,128)(2,1)S(1)}, bf16[1024,128]{1,0:T(8,128)(2,1)S(1)}, u32[]{:S(2)}, u32[]{:S(2)}) collective-permute-start(bf16[1024,128]{1,0:T(8,128)(2,1)S(1)} %collective-permute-done.7), channel_id=1, source_target_pairs={{0,64},{16,80},{32,96},{48,112},{64,0},{80,16},{96,32},{112,48},{1... | collective-permute-start | bytes 786440 | tf_op jit(solution)/shard_map/ppermute | solution.py:32
  105.8 39.6 %collective-permute-start.17 = (bf16[1024,128]{1,0:T(8,128)(2,1)S(1)}, bf16[1024,128]{1,0:T(8,128)(2,1)S(1)}, u32[]{:S(2)}, u32[]{:S(2)}) collective-permute-start(bf16[1024,128]{1,0:T(8,128)(2,1)S(1)} %collective-permute-done.13), channel_id=1, source_target_pairs={{0,16},{16,32},{32,48},{48,64},{64,80},{80,96},{96,112},{112,0},{1... | collective-permute-start | bytes 786440 | tf_op jit(solution)/shard_map/ppermute | solution.py:38
  110.6 34.7 %collective-permute-start.19 = (bf16[1024,128]{1,0:T(8,128)(2,1)S(1)}, bf16[1024,128]{1,0:T(8,128)(2,1)S(1)}, u32[]{:S(2)}, u32[]{:S(2)}) collective-permute-start(bf16[1024,128]{1,0:T(8,128)(2,1)S(1)} %collective-permute-done.15), channel_id=1, source_target_pairs={{0,16},{16,32},{32,48},{48,64},{64,80},{80,96},{96,112},{112,0},{1... | collective-permute-start | bytes 786440 | tf_op jit(solution)/shard_map/ppermute | solution.py:38
  112.7 39.3 %collective-permute-start.5 = (bf16[512,3,128]{2,0,1:T(8,128)(2,1)S(1)}, bf16[512,3,128]{2,0,1:T(8,128)(2,1)S(1)}, u32[]{:S(2)}, u32[]{:S(2)}) collective-permute-start(bf16[512,3,128]{2,0,1:T(8,128)(2,1)S(1)} %collective-permute-done.4), channel_id=1, source_target_pairs={{0,64},{16,80},{32,96},{48,112},{64,0},{80,16},{96,32},{112,48},{1... | collective-permute-start | bytes 1179656 | tf_op jit(solution)/shard_map/ppermute | solution.py:32
  125.7 37.5 %collective-permute-start.10 = (bf16[1024,128]{1,0:T(8,128)(2,1)S(1)}, bf16[1024,128]{1,0:T(8,128)(2,1)S(1)}, u32[]{:S(2)}, u32[]{:S(2)}) collective-permute-start(bf16[1024,128]{1,0:T(8,128)(2,1)S(1)} %collective-permute-done.2), channel_id=1, source_target_pairs={{0,16},{16,32},{32,48},{48,64},{64,80},{80,96},{96,112},{112,0},{1... | collective-permute-start | bytes 786440 | tf_op jit(solution)/shard_map/ppermute | solution.py:38
  145.3 20.3 %collective-permute-start.12 = (bf16[1024,128]{1,0:T(8,128)(2,1)S(1)}, bf16[1024,128]{1,0:T(8,128)(2,1)S(1)}, u32[]{:S(2)}, u32[]{:S(2)}) collective-permute-start(bf16[1024,128]{1,0:T(8,128)(2,1)S(1)} %collective-permute-done.8), channel_id=1, source_target_pairs={{0,16},{16,32},{32,48},{48,64},{64,80},{80,96},{96,112},{112,0},{1... | collective-permute-start | bytes 786440 | tf_op jit(solution)/shard_map/ppermute | solution.py:38
  145.3 27.4 %collective-permute-start.21 = (bf16[1024,128]{1,0:T(8,128)(2,1)S(1)}, bf16[1024,128]{1,0:T(8,128)(2,1)S(1)}, u32[]{:S(2)}, u32[]{:S(2)}) collective-permute-start(bf16[1024,128]{1,0:T(8,128)(2,1)S(1)} %collective-permute-done.17), channel_id=1, source_target_pairs={{0,16},{16,32},{32,48},{48,64},{64,80},{80,96},{96,112},{112,0},{1... | collective-permute-start | bytes 786440 | tf_op jit(solution)/shard_map/ppermute | solution.py:38
  145.4 27.7 %collective-permute-start.23 = (bf16[1024,128]{1,0:T(8,128)(2,1)S(1)}, bf16[1024,128]{1,0:T(8,128)(2,1)S(1)}, u32[]{:S(2)}, u32[]{:S(2)}) collective-permute-start(bf16[1024,128]{1,0:T(8,128)(2,1)S(1)} %collective-permute-done.19), channel_id=1, source_target_pairs={{0,16},{16,32},{32,48},{48,64},{64,80},{80,96},{96,112},{112,0},{1... | collective-permute-start | bytes 786440 | tf_op jit(solution)/shard_map/ppermute | solution.py:38
  169.6 12.9 %collective-permute-start.14 = (bf16[1024,128]{1,0:T(8,128)(2,1)S(1)}, bf16[1024,128]{1,0:T(8,128)(2,1)S(1)}, u32[]{:S(2)}, u32[]{:S(2)}) collective-permute-start(bf16[1024,128]{1,0:T(8,128)(2,1)S(1)} %collective-permute-done.10), channel_id=1, source_target_pairs={{0,16},{16,32},{32,48},{48,64},{64,80},{80,96},{96,112},{112,0},{1... | collective-permute-start | bytes 786440 | tf_op jit(solution)/shard_map/ppermute | solution.py:38
  172.6 15.5 %collective-permute-start.16 = (bf16[1024,128]{1,0:T(8,128)(2,1)S(1)}, bf16[1024,128]{1,0:T(8,128)(2,1)S(1)}, u32[]{:S(2)}, u32[]{:S(2)}) collective-permute-start(bf16[1024,128]{1,0:T(8,128)(2,1)S(1)} %collective-permute-done.12), channel_id=1, source_target_pairs={{0,16},{16,32},{32,48},{48,64},{64,80},{80,96},{96,112},{112,0},{1... | collective-permute-start | bytes 786440 | tf_op jit(solution)/shard_map/ppermute | solution.py:38
  172.8 20.9 %collective-permute-start.25 = (bf16[1024,128]{1,0:T(8,128)(2,1)S(1)}, bf16[1024,128]{1,0:T(8,128)(2,1)S(1)}, u32[]{:S(2)}, u32[]{:S(2)}) collective-permute-start(bf16[1024,128]{1,0:T(8,128)(2,1)S(1)} %collective-permute-done.21), channel_id=1, source_target_pairs={{0,16},{16,32},{32,48},{48,64},{64,80},{80,96},{96,112},{112,0},{1... | collective-permute-start | bytes 786440 | tf_op jit(solution)/shard_map/ppermute | solution.py:38
  173.0 26.3 %collective-permute-start.27 = (bf16[1024,128]{1,0:T(8,128)(2,1)S(1)}, bf16[1024,128]{1,0:T(8,128)(2,1)S(1)}, u32[]{:S(2)}, u32[]{:S(2)}) collective-permute-start(bf16[1024,128]{1,0:T(8,128)(2,1)S(1)} %collective-permute-done.23), channel_id=1, source_target_pairs={{0,16},{16,32},{32,48},{48,64},{64,80},{80,96},{96,112},{112,0},{1... | collective-permute-start | bytes 786440 | tf_op jit(solution)/shard_map/ppermute | solution.py:38
  192.0 12.9 %collective-permute-start.18 = (bf16[1024,128]{1,0:T(8,128)(2,1)S(1)}, bf16[1024,128]{1,0:T(8,128)(2,1)S(1)}, u32[]{:S(2)}, u32[]{:S(2)}) collective-permute-start(bf16[1024,128]{1,0:T(8,128)(2,1)S(1)} %collective-permute-done.14), channel_id=1, source_target_pairs={{0,16},{16,32},{32,48},{48,64},{64,80},{80,96},{96,112},{112,0},{1... | collective-permute-start | bytes 786440 | tf_op jit(solution)/shard_map/ppermute | solution.py:38
  193.6 17.0 %collective-permute-start.20 = (bf16[1024,128]{1,0:T(8,128)(2,1)S(1)}, bf16[1024,128]{1,0:T(8,128)(2,1)S(1)}, u32[]{:S(2)}, u32[]{:S(2)}) collective-permute-start(bf16[1024,128]{1,0:T(8,128)(2,1)S(1)} %collective-permute-done.16), channel_id=1, source_target_pairs={{0,16},{16,32},{32,48},{48,64},{64,80},{80,96},{96,112},{112,0},{1... | collective-permute-start | bytes 786440 | tf_op jit(solution)/shard_map/ppermute | solution.py:38
  193.7 22.5 %collective-permute-start.29 = (bf16[1024,128]{1,0:T(8,128)(2,1)S(1)}, bf16[1024,128]{1,0:T(8,128)(2,1)S(1)}, u32[]{:S(2)}, u32[]{:S(2)}) collective-permute-start(bf16[1024,128]{1,0:T(8,128)(2,1)S(1)} %collective-permute-done.25), channel_id=1, source_target_pairs={{0,16},{16,32},{32,48},{48,64},{64,80},{80,96},{96,112},{112,0},{1... | collective-permute-start | bytes 786440 | tf_op jit(solution)/shard_map/ppermute | solution.py:38
  199.3 22.5 %collective-permute-start.31 = (bf16[1024,128]{1,0:T(8,128)(2,1)S(1)}, bf16[1024,128]{1,0:T(8,128)(2,1)S(1)}, u32[]{:S(2)}, u32[]{:S(2)}) collective-permute-start(bf16[1024,128]{1,0:T(8,128)(2,1)S(1)} %collective-permute-done.27), channel_id=1, source_target_pairs={{0,16},{16,32},{32,48},{48,64},{64,80},{80,96},{96,112},{112,0},{1... | collective-permute-start | bytes 786440 | tf_op jit(solution)/shard_map/ppermute | solution.py:38
  214.5 12.9 %collective-permute-start.22 = (bf16[1024,128]{1,0:T(8,128)(2,1)S(1)}, bf16[1024,128]{1,0:T(8,128)(2,1)S(1)}, u32[]{:S(2)}, u32[]{:S(2)}) collective-permute-start(bf16[1024,128]{1,0:T(8,128)(2,1)S(1)} %collective-permute-done.18), channel_id=1, source_target_pairs={{0,16},{16,32},{32,48},{48,64},{64,80},{80,96},{96,112},{112,0},{1... | collective-permute-start | bytes 786440 | tf_op jit(solution)/shard_map/ppermute | solution.py:38
  216.0 17.0 %collective-permute-start.24 = (bf16[1024,128]{1,0:T(8,128)(2,1)S(1)}, bf16[1024,128]{1,0:T(8,128)(2,1)S(1)}, u32[]{:S(2)}, u32[]{:S(2)}) collective-permute-start(bf16[1024,128]{1,0:T(8,128)(2,1)S(1)} %collective-permute-done.20), channel_id=1, source_target_pairs={{0,16},{16,32},{32,48},{48,64},{64,80},{80,96},{96,112},{112,0},{1... | collective-permute-start | bytes 786440 | tf_op jit(solution)/shard_map/ppermute | solution.py:38
  216.2 61.4 %collective-permute-start.33 = (bf16[1024,128]{1,0:T(8,128)(2,1)S(1)}, bf16[1024,128]{1,0:T(8,128)(2,1)S(1)}, u32[]{:S(2)}, u32[]{:S(2)}) collective-permute-start(bf16[1024,128]{1,0:T(8,128)(2,1)S(1)} %collective-permute-done.29), channel_id=1, source_target_pairs={{0,16},{16,32},{32,48},{48,64},{64,80},{80,96},{96,112},{112,0},{1... | collective-permute-start | bytes 786440 | tf_op jit(solution)/shard_map/ppermute | solution.py:38
  221.8 67.7 %collective-permute-start.35 = (bf16[1024,128]{1,0:T(8,128)(2,1)S(1)}, bf16[1024,128]{1,0:T(8,128)(2,1)S(1)}, u32[]{:S(2)}, u32[]{:S(2)}) collective-permute-start(bf16[1024,128]{1,0:T(8,128)(2,1)S(1)} %collective-permute-done.31), channel_id=1, source_target_pairs={{0,16},{16,32},{32,48},{48,64},{64,80},{80,96},{96,112},{112,0},{1... | collective-permute-start | bytes 786440 | tf_op jit(solution)/shard_map/ppermute | solution.py:38
  236.9 12.9 %collective-permute-start.26 = (bf16[1024,128]{1,0:T(8,128)(2,1)S(1)}, bf16[1024,128]{1,0:T(8,128)(2,1)S(1)}, u32[]{:S(2)}, u32[]{:S(2)}) collective-permute-start(bf16[1024,128]{1,0:T(8,128)(2,1)S(1)} %collective-permute-done.22), channel_id=1, source_target_pairs={{0,16},{16,32},{32,48},{48,64},{64,80},{80,96},{96,112},{112,0},{1... | collective-permute-start | bytes 786440 | tf_op jit(solution)/shard_map/ppermute | solution.py:38
  238.5 14.3 %collective-permute-start.28 = (bf16[1024,128]{1,0:T(8,128)(2,1)S(1)}, bf16[1024,128]{1,0:T(8,128)(2,1)S(1)}, u32[]{:S(2)}, u32[]{:S(2)}) collective-permute-start(bf16[1024,128]{1,0:T(8,128)(2,1)S(1)} %collective-permute-done.24), channel_id=1, source_target_pairs={{0,16},{16,32},{32,48},{48,64},{64,80},{80,96},{96,112},{112,0},{1... | collective-permute-start | bytes 786440 | tf_op jit(solution)/shard_map/ppermute | solution.py:38
  256.8 12.2 %collective-permute-start.30 = (bf16[1024,128]{1,0:T(8,128)(2,1)S(1)}, bf16[1024,128]{1,0:T(8,128)(2,1)S(1)}, u32[]{:S(2)}, u32[]{:S(2)}) collective-permute-start(bf16[1024,128]{1,0:T(8,128)(2,1)S(1)} %collective-permute-done.26), channel_id=1, source_target_pairs={{0,16},{16,32},{32,48},{48,64},{64,80},{80,96},{96,112},{112,0},{1... | collective-permute-start | bytes 786440 | tf_op jit(solution)/shard_map/ppermute | solution.py:38
  258.3 13.4 %collective-permute-start.32 = (bf16[1024,128]{1,0:T(8,128)(2,1)S(1)}, bf16[1024,128]{1,0:T(8,128)(2,1)S(1)}, u32[]{:S(2)}, u32[]{:S(2)}) collective-permute-start(bf16[1024,128]{1,0:T(8,128)(2,1)S(1)} %collective-permute-done.28), channel_id=1, source_target_pairs={{0,16},{16,32},{32,48},{48,64},{64,80},{80,96},{96,112},{112,0},{1... | collective-permute-start | bytes 786440 | tf_op jit(solution)/shard_map/ppermute | solution.py:38
  275.7 11.3 %collective-permute-start.34 = (bf16[1024,128]{1,0:T(8,128)(2,1)S(1)}, bf16[1024,128]{1,0:T(8,128)(2,1)S(1)}, u32[]{:S(2)}, u32[]{:S(2)}) collective-permute-start(bf16[1024,128]{1,0:T(8,128)(2,1)S(1)} %collective-permute-done.30), channel_id=1, source_target_pairs={{0,16},{16,32},{32,48},{48,64},{64,80},{80,96},{96,112},{112,0},{1... | collective-permute-start | bytes 786440 | tf_op jit(solution)/shard_map/ppermute | solution.py:38
  277.2 12.5 %collective-permute-start.36 = (bf16[1024,128]{1,0:T(8,128)(2,1)S(1)}, bf16[1024,128]{1,0:T(8,128)(2,1)S(1)}, u32[]{:S(2)}, u32[]{:S(2)}) collective-permute-start(bf16[1024,128]{1,0:T(8,128)(2,1)S(1)} %collective-permute-done.32), channel_id=1, source_target_pairs={{0,16},{16,32},{32,48},{48,64},{64,80},{80,96},{96,112},{112,0},{1... | collective-permute-start | bytes 786440 | tf_op jit(solution)/shard_map/ppermute | solution.py:38
  295.5 11.2 %collective-permute-start.37 = (bf16[512,384]{0,1:T(8,128)(2,1)S(1)}, bf16[512,384]{0,1:T(8,128)(2,1)S(1)}, u32[]{:S(2)}, u32[]{:S(2)}) collective-permute-start(bf16[512,384]{0,1:T(8,128)(2,1)S(1)} %fusion.269), channel_id=1, source_target_pairs={{0,16},{16,0},{32,48},{48,32},{64,80},{80,64},{96,112},{112,96},{1... | collective-permute-start | bytes 1179656 | tf_op jit(solution)/shard_map/ppermute | solution.py:32
  306.7 9.3 %collective-permute-start.38 = (bf16[512,384]{0,1:T(8,128)(2,1)S(1)}, bf16[512,384]{0,1:T(8,128)(2,1)S(1)}, u32[]{:S(2)}, u32[]{:S(2)}) collective-permute-start(bf16[512,384]{0,1:T(8,128)(2,1)S(1)} %collective-permute-done.37), channel_id=1, source_target_pairs={{0,32},{16,48},{32,0},{48,16},{64,96},{80,112},{96,64},{112,80},{1... | collective-permute-start | bytes 1179656 | tf_op jit(solution)/shard_map/ppermute | solution.py:32
  316.0 10.5 %collective-permute-start.39 = (bf16[512,384]{0,1:T(8,128)(2,1)S(1)}, bf16[512,384]{0,1:T(8,128)(2,1)S(1)}, u32[]{:S(2)}, u32[]{:S(2)}) collective-permute-start(bf16[512,384]{0,1:T(8,128)(2,1)S(1)} %collective-permute-done.38), channel_id=1, source_target_pairs={{0,64},{16,80},{32,96},{48,112},{64,0},{80,16},{96,32},{112,48},{1... | collective-permute-start | bytes 1179656 | tf_op jit(solution)/shard_map/ppermute | solution.py:32
  337.1 6.4 copy-start.24
  337.1 175.1 %all-to-all-start.2 = ((bf16[16,1024,384]{2,1,0:T(8,128)(2,1)}), bf16[16,1024,384]{2,1,0:T(8,128)(2,1)}, u32[]{:S(2)}, u32[]{:S(2)}) async-start(bf16[16,1024,384]{2,1,0:T(8,128)(2,1)} %stack.11), calls=%async_computation.2 | async-start | bytes 25165824 | tf_op jit(solution)/shard_map/all_to_all | solution.py:233
  342.8 179.2 %all-gather.2.cloned.1.call-start = ((), (), s32[]{:S(2)}) async-start(), calls=%async_computation.6 | async-start | bytes 2654208 | tf_op jit(solution)/shard_map/all_gather | solution.py:227
  521.9 2.3 copy-start.18
  524.2 1.7 copy-start.17
  532.6 1.7 copy-start.5
  532.7 3.3 copy-start.12
  536.0 2.0 copy-start.11
  550.9 6.2 copy-start.23
  552.4 25.7 %all-to-all-start.3 = ((bf16[16,128,384]{2,1,0:T(8,128)(2,1)}), bf16[16,128,384]{2,1,0:T(8,128)(2,1)}, u32[]{:S(2)}, u32[]{:S(2)}) async-start(bf16[16,128,384]{2,1,0:T(8,128)(2,1)} %copy.257), calls=%async_computation.3 | async-start | bytes 3145728 | tf_op jit(solution)/shard_map/all_to_all | solution.py:251
  580.7 2.9 copy-start.1
  580.7 2.9 copy-start.2
  668.2 3.5 collective-permute-start.40
  676.8 5.5 copy-start.25
  684.7 2.0 collective-permute-start.41
  694.1 7.8 copy-start.22
  694.1 60.1 %all-to-all-start.5 = ((bf16[16,33,3072]{2,1,0:T(8,128)(2,1)}), bf16[16,33,3072]{2,1,0:T(8,128)(2,1)}, u32[]{:S(2)}, u32[]{:S(2)}) async-start(bf16[16,33,3072]{2,1,0:T(8,128)(2,1)} %reshape.775), calls=%async_computation.5 | async-start | bytes 7864320 | tf_op jit(solution)/shard_map/all_to_all | solution.py:301
  (10 other events, 17.0 us)
Sparse Core Ops, SparseCore 0:
  345.9 159.4 all-gather.1
